TPU v7x, 1024 devices: a whole 8x8x8 slice. The times are simulated.
1024 devices in a mesh: row: 64 (over x, z), col: 16 (over y, core).
Axes of the slice: x: 8, y: 8, z: 8, core: 2. Of those that a mesh axis runs over, the one named last changes fastest.
Arguments:
- rhs: bfloat16 [2, 32768, 8192], P(None, 'row', 'col'), may hold values from -6 to 6
- panel: bfloat16 [2, 32768, 1024], P(None, 'row', 'col'), may hold values from -0.25 to 0.25
- pivots: float32 [1024], P('col'), may hold values from 2 to 4
Outputs:
- updated: float32 [2, 32768, 8192], P(None, 'row', 'col')
All inputs are finite; a program needn't handle non-finite values.
Results may differ from a plain program's by a relative error of at most 0.0045.
Values may be sent and summed in bfloat16 or wider, within the bound.
A program may use at most 32 MiB of HBM per device.

v0:
```python
import jax
import jax.numpy as jnp
from jax import lax
from jax.sharding import Mesh
from jax.sharding import PartitionSpec as P

ROW = ("row_0", "row_1")
COL = ("col_0", "col_1")


def whole_of(x, axes, dim):
    for axis in reversed(axes):
        x = lax.all_gather(x, axis, axis=dim, tiled=True)
    return x


def from_root(x, axes, root):
    x = jnp.where(lax.axis_index(axes) == root, x, jnp.zeros_like(x))
    for axis in axes:
        x = lax.psum(x, axis)
    return x


def lower_solve(matrix, values):
    return lax.linalg.triangular_solve(matrix, values, left_side=True, lower=True)


def diagonal_tile(tile_rows, pivots_all, step):
    width = tile_rows.shape[0]
    strict = jnp.tril(tile_rows[:, step * width : (step + 1) * width].astype(jnp.float32), -1)
    return strict + jnp.diag(pivots_all[step * width : (step + 1) * width])


def on_device(rhs, panel, pivots):
    layers = rhs.shape[0]
    width = rhs.shape[1]
    columns = rhs.shape[2]
    row_index = lax.axis_index(ROW)
    whole, pivots_all = (
        whole_of(panel, COL, 2),
        whole_of(pivots.astype(jnp.bfloat16), COL, 0).astype(pivots.dtype),
    )
    left = whole.reshape(layers * width, 2 * width)
    received = []
    for step in range(2):
        received.append((from_root(rhs[0], ROW, step), from_root(whole[0], ROW, step)))
    first = lower_solve(
        diagonal_tile(received[0][1], pivots_all, 0), received[0][0].astype(jnp.float32)
    )
    first_low = first.astype(jnp.bfloat16)
    second_side = received[1][0].astype(jnp.float32) - jnp.dot(
        received[1][1][:, 0:width], first_low, preferred_element_type=jnp.float32
    )
    second = lower_solve(diagonal_tile(received[1][1], pivots_all, 1), second_side)
    second_low = second.astype(jnp.bfloat16)
    both_low = jnp.concatenate([first_low, second_low], axis=0)
    product = jnp.dot(left, both_low, preferred_element_type=jnp.float32).reshape(
        layers, width, columns
    )
    current = rhs.astype(jnp.float32) - product
    head = jnp.where(row_index == 0, first, jnp.where(row_index == 1, second, current[0]))
    return current.at[0].set(head)


def solution(mesh):
    torus = Mesh(mesh.devices.reshape(8, 8, 8, 2), ("row_0", "row_1", "col_0", "col_1"))
    return jax.shard_map(
        on_device,
        mesh=torus,
        in_specs=(P(None, ROW, COL), P(None, ROW, COL), P(COL)),
        out_specs=P(None, ROW, COL),
        check_vma=False,
    )
```

profile of v0, /device:TPU:1, one launch (start us, length us, event | category | flops | bytes accessed | tf_op | source)
XLA Modules:
  0.0 415.0 jit_solution(8272053397215637535)
XLA Ops:
  7.6 15.7 %all_gather.12 = bf16[2,512,128]{1,0,2:T(2,128)(2,1)S(1)} all-gather(bf16[2,512,64]{1,0,2:T(2,128)(2,1)S(1)} %copy.12), channel_id=1, replica_groups=mesh['row_0'=8,'row_1'=8,'col_0'=8,'col_1'=2] {'col_1'}, dimensions={2}, use_global_device_ids=true | all-gather | bytes 393216 | tf_op jit(solution)/shard_map/all_gather | solution.py:13
  24.3 2.1 select_bitcast_fusion.2
  26.4 44.3 %all-gather.3.cloned.1.call-done = bf16[2,512,1024]{2,1,0:T(8,128)(2,1)} async-done(((bf16[2,512,128]{2,1,0:T(8,128)(2,1)}), bf16[2,512,1024]{2,1,0:T(8,128)(2,1)}) %all-gather.3.cloned.1.call-update) | async-done | bytes 2097168 | tf_op jit(solution)/shard_map/all_gather | solution.py:13
  70.7 2.7 select_bitcast_fusion
  73.5 106.2 %all-reduce.8.cloned.1.call-done = (bf16[512,512]{1,0:T(8,128)(2,1)}, bf16[512,1024]{1,0:T(8,128)(2,1)}, bf16[512,512]{1,0:T(8,128)(2,1)}, bf16[512,1024]{1,0:T(8,128)(2,1)}) async-done(((bf16[512,512]{1,0:T(8,128)(2,1)}, bf16[512,1024]{1,0:T(8,128)(2,1)}, bf16[512,512]{1,0:T(8,128)(2,1)}, bf16[512,1024]{1,0:T(8,128)(2,1)}), (bf16[512,512]{1,0:T(8,128)(2,1)}, bf16[512,1024]{1,0:T(8,128)(2,1)}, ...) | async-done | bytes 3145744 | tf_op jit(solution)/shard_map/psum | solution.py:20
  182.0 3.6 all-reduce
  185.5 12.5 %all-gather = bf16[8,1,128]{2,1,0:T(2,128)(2,1)S(1)} all-gather(bf16[1,1,128]{2,1,0:T(2,128)(2,1)S(1)} %bitcast.88), channel_id=1, replica_groups=mesh['row_0'=8,'row_1'=8,'col_0'=8,'col_1'=2] {'col_0'}, dimensions={0}, use_global_device_ids=true | all-gather | bytes 2304 | tf_op jit(solution)/shard_map/all_gather | solution.py:13
  198.1 89.7 %all-reduce.6.cloned.1.call-done = (bf16[512,512]{1,0:T(8,128)(2,1)}, bf16[512,1024]{1,0:T(8,128)(2,1)}, bf16[512,512]{1,0:T(8,128)(2,1)}, bf16[512,1024]{1,0:T(8,128)(2,1)}) async-done(((bf16[512,512]{1,0:T(8,128)(2,1)}, bf16[512,1024]{1,0:T(8,128)(2,1)}, bf16[512,512]{1,0:T(8,128)(2,1)}, bf16[512,1024]{1,0:T(8,128)(2,1)}), (bf16[512,512]{1,0:T(8,128)(2,1)}, bf16[512,1024]{1,0:T(8,128)(2,1)}, ...) | async-done | bytes 3145744 | tf_op jit(solution)/shard_map/psum | solution.py:20
  287.8 1.6 fusion.7
  289.5 8.0 %while.5 = (s32[]{:T(128)}, f32[512,512]{1,0:T(8,128)S(1)}, s32[4,2]{0,1:T(2,128)S(1)}, f32[4,128,128]{2,1,0:T(8,128)S(1)}, s32[]{:T(128)}) while((s32[]{:T(128)}, f32[512,512]{1,0:T(8,128)S(1)}, s32[4,2]{0,1:T(2,128)S(1)}, f32[4,128,128]{2,1,0:T(8,128)S(1)}, s32[]{:T(128)}) %tuple.45), condition=%wide.while_cond.1, body=%wide.while_body.1.sunk | while | flops 2 | bytes 131181 | solution.py:25
  290.1 1.4 bitcast_dynamic-update-slice_fusion.4
  292.1 1.4 bitcast_dynamic-update-slice_fusion.4
  294.1 1.4 bitcast_dynamic-update-slice_fusion.4
  296.1 1.4 bitcast_dynamic-update-slice_fusion.4
  297.5 39.3 %custom-call.4 = f32[4,128,128]{1,2,0:T(8,128)S(1)} custom-call(f32[4,128,128]{2,1,0:T(8,128)S(1)} %get-tuple-element.32), custom_call_target="InvertDiagBlocksLowerTriangular" | custom-call | tf_op jit(solution)/shard_map/triangular_solve/custom-call.1 | solution.py:25
  341.2 8.0 %while.6 = (s32[]{:T(128)}, f32[512,512]{1,0:T(8,128)S(1)}, s32[4,2]{0,1:T(2,128)S(1)}, f32[4,128,128]{2,1,0:T(8,128)S(1)}, s32[]{:T(128)}) while((s32[]{:T(128)}, f32[512,512]{1,0:T(8,128)S(1)}, s32[4,2]{0,1:T(2,128)S(1)}, f32[4,128,128]{2,1,0:T(8,128)S(1)}, s32[]{:T(128)}) %tuple.59), condition=%wide.while_cond.1.clone, body=%wide.while_body.1.clone.sunk | while | flops 2 | bytes 131181 | solution.py:25
  341.8 1.3 bitcast_dynamic-update-slice_fusion.5
  349.9 40.1 %custom-call.5 = f32[4,128,128]{1,2,0:T(8,128)S(1)} custom-call(f32[4,128,128]{2,1,0:T(8,128)} %copy-done.11), custom_call_target="InvertDiagBlocksLowerTriangular" | custom-call | tf_op jit(solution)/shard_map/triangular_solve/custom-call.1 | solution.py:25
  390.1 1.6 convolution_subtract_fusion
  394.1 1.4 fusion.37
  398.3 2.6 convolution_bitcast_fusion
  400.9 1.9 copy.14
  402.9 3.0 convert_subtract_fusion
  405.9 2.6 fusion.3
  (79 shorter events, 22.7 us)
Async XLA Ops:
  6.5 64.2 %all-gather.3.cloned.1.call-start = ((), (), s32[]{:S(2)}) async-start(), calls=%async_computation | async-start | bytes 2359296 | tf_op jit(solution)/shard_map/all_gather | solution.py:13
  24.2 155.5 %all-reduce.8.cloned.1.call-start = ((), (), s32[]{:S(2)}) async-start(), calls=%async_computation.2 | async-start | bytes 6291456 | tf_op jit(solution)/shard_map/psum | solution.py:20
  73.4 106.3 %copy-start.12 = (f32[64]{0:T(128)S(1)}, f32[64]{0:T(128)}, u32[]{:S(2)}) copy-start(f32[64]{0:T(128)} %param.9) | copy-start | bytes 772
  73.4 214.3 %all-reduce.6.cloned.1.call-start = ((), (), s32[]{:S(2)}) async-start(), calls=%async_computation.1 | async-start | bytes 6291456 | tf_op jit(solution)/shard_map/psum | solution.py:20
  287.8 49.1 %copy-start.7 = (bf16[512,512]{1,0:T(8,128)(2,1)S(1)}, bf16[512,512]{1,0:T(8,128)(2,1)}, u32[]{:S(2)}) copy-start(bf16[512,512]{1,0:T(8,128)(2,1)} %get-tuple-element.58) | copy-start | bytes 1572868
  336.9 1.8 copy-start.10
  339.8 50.3 %copy-start.6 = (bf16[512,512]{1,0:T(8,128)(2,1)S(1)}, bf16[512,512]{1,0:T(8,128)(2,1)}, u32[]{:S(2)}) copy-start(bf16[512,512]{1,0:T(8,128)(2,1)} %get-tuple-element.60) | copy-start | bytes 1572868
  341.1 48.9 %copy-start.2 = (f32[128,512]{1,0:T(8,128)}, f32[128,512]{1,0:T(8,128)S(1)}, u32[]{:S(2)}) copy-start(f32[128,512]{1,0:T(8,128)S(1)} %fusion.40) | copy-start | bytes 786436
  349.2 0.7 copy-start.11
  390.0 2.0 copy-start.9
  394.1 4.1 copy-start.8
  395.6 2.7 copy-start
  397.5 0.7 copy-start.4
  402.8 3.0 copy-start.1
  402.8 3.0 copy-start.3
  402.8 3.0 copy-start.5
Sparse Core Ops, SparseCore 0:
  24.4 46.2 all-gather.2
  73.6 106.1 all-reduce.7
  182.3 105.3 all-reduce.5
where the time goes:
time: 416 us; the launch traced here: 415 us
  waiting for transfers between devices  240 us (58%)
  other arithmetic  91.8 us (22%)
  blocking collectives  31.8 us (8%)
  local copies, waits for them, and re-layouts  22.7 us (5%)
  between operations  14.2 us (3%)
  matrix products  14 us (3%)
    psum x2, waiting for transfers between devices, from_root(): x = lax.psum(x, axis)  196 us
    another operation x4, other arithmetic, lower_solve(): lax.linalg.triangular_solve(matrix, values, left_side=True, lower=True)  81.1 us
    all_gather x1, waiting for transfers between devices, whole_of(): x = lax.all_gather(x, axis, axis=dim, tiled=True)  44.3 us
    all_gather x2, blocking collectives, whole_of(): x = lax.all_gather(x, axis, axis=dim, tiled=True)  28.3 us
    another operation x27, local copies, waits for them, and re-layouts, lower_solve(): lax.linalg.triangular_solve(matrix, values, left_side=True, lower=True)  15.9 us
    another operation x14, matrix products, lower_solve(): lax.linalg.triangular_solve(matrix, values, left_side=True, lower=True)  9.78 us
  transfers between devices with their start and end apart: 3, of which 3 were waited for; matrix products, arithmetic and copies ran while one was open for 1% of the time, Pallas kernels for 0%

commit v1 on v0

v1 whole, which is shorter than its diff:
```python
import functools

import jax
import jax.numpy as jnp
from jax import lax
from jax.experimental import pallas as pl
from jax.experimental.pallas import tpu as pltpu
from jax.sharding import Mesh
from jax.sharding import PartitionSpec as P

MESH = pl.DeviceIdType.MESH
F32 = jnp.float32
BF16 = jnp.bfloat16
X, Z, Y, CORE = "row_0", "row_1", "col_0", "col_1"
RING = 8
PLANE, RIDGE = 1, 0
ROUNDS = 8
DEEP = 256 // ROUNDS
LAG = 3


def dot(a, b):
    return jnp.dot(a, b, preferred_element_type=F32)


def split(v):
    high = v.astype(BF16)
    return high, (v - high.astype(F32)).astype(BF16)


def dot_exact_left(a, b):
    high, low = split(b)
    return dot(a, high) + dot(a, low)


def dot_exact_right(a, b):
    high, low = split(a)
    return dot(high, b) + dot(low, b)


def dot_both(a, b):
    ah, al = split(a)
    bh, bl = split(b)
    return dot(ah, bh) + (dot(ah, bl) + dot(al, bh))


def iota(shape, dim):
    return lax.broadcasted_iota(jnp.int32, shape, dim)


def invert_diagonal(block, pivots):
    n, base = 128, 32
    rows, cols = iota((n, n), 0), iota((n, n), 1)
    raw = jnp.where(rows > cols, block.astype(F32), 0.0)
    inverse_row = 1.0 / pivots
    inverse_col = jnp.sum(jnp.where(rows == cols, inverse_row, 0.0), axis=1, keepdims=True)
    scaled = raw * inverse_col
    parts = []
    for at in range(0, n, base):
        lower = scaled[at : at + base, :]
        part = (iota((base, n), 0) + at == iota((base, n), 1)).astype(F32)
        for j in range(base - 1):
            part = part - lower[:, at + j : at + j + 1] * part[j : j + 1, :]
        parts.append(part)
    result = jnp.concatenate(parts, axis=0)
    inside = rows // base == cols // base
    result = jnp.where(inside, result, 0.0) * inverse_row
    size = base
    while size < n:
        below = (rows // size) % 2 == 1
        mask = below & (cols // size == rows // size - 1)
        link = jnp.where(mask, raw, 0.0).astype(BF16)
        result = result - dot_both(result, dot_exact_left(link, result))
        size *= 2
    return result


def kernel(
    rhs_hbm, panel_hbm, pivots_hbm, out_hbm,
    own, sibling_own, piv, sibling_piv, rhs, panel, sides, slabs, inverses, low, full, out,
    local_sem, pair_send, pair_recv,
    plane_send, plane_recv, hand_send, hand_recv,
    p_send, p_recv, p_hand_send, p_hand_recv,
    s_send, s_recv, s_hand_send, s_hand_recv,
):
    x, z, y, core = (lax.axis_index(name) for name in (X, Z, Y, CORE))
    row = x * RING + z
    is_plane = core == PLANE
    is_ridge = core == RIDGE

    def around(value, by):
        return lax.rem(value + by + RING, RING)

    def remote(src, dst, send, recv, where):
        return pltpu.make_async_remote_copy(
            src_ref=src, dst_ref=dst, send_sem=send, recv_sem=recv, device_id=where, device_id_type=MESH
        )

    mate = {CORE: 1 - core}

    take_panel = pltpu.make_async_copy(panel_hbm, own, local_sem.at[0])
    take_piv = pltpu.make_async_copy(pivots_hbm, piv, local_sem.at[1])
    take_rhs = pltpu.make_async_copy(rhs_hbm, rhs, local_sem.at[2])
    take_panel.start()
    take_piv.start()
    take_rhs.start()
    barrier = pltpu.get_barrier_semaphore()
    pl.semaphore_signal(barrier, inc=1, device_id=mate, device_id_type=MESH)

    @pl.when(is_plane)
    def _():
        for by in (1, -1):
            pl.semaphore_signal(barrier, inc=1, device_id={X: around(x, by)}, device_id_type=MESH)
            pl.semaphore_signal(barrier, inc=1, device_id={Z: around(z, by)}, device_id_type=MESH)
        pl.semaphore_wait(barrier, 5)

    @pl.when(is_ridge)
    def _():
        for by in (1, -1):
            pl.semaphore_signal(barrier, inc=1, device_id={Y: around(y, by)}, device_id_type=MESH)
        pl.semaphore_wait(barrier, 3)

    take_panel.wait()
    pair_panel = remote(own, sibling_own, pair_send.at[0], pair_recv.at[0], mate)
    pair_panel.start()
    take_piv.wait()
    pair_piv = remote(piv, sibling_piv, pair_send.at[1], pair_recv.at[1], mate)
    pair_piv.start()
    take_rhs.wait()
    pair_side = remote(rhs.at[0], sides.at[RIDGE, row], pair_send.at[2], pair_recv.at[2], mate)

    @pl.when((row < 2) & is_ridge)
    def _():
        pair_side.start()

    pair_panel.wait_recv()
    lane, place = iota((64, 128), 1), iota((64, 128), 0)
    mine = (lane == place + core * 64).astype(BF16)
    theirs = (lane == place + (1 - core) * 64).astype(BF16)
    for layer in range(2):
        chip = (dot(own[layer], mine) + dot(sibling_own[layer], theirs)).astype(BF16)
        panel[y, layer * 512 : (layer + 1) * 512, :] = chip

    def needed(kind, tile, tree, at):
        if kind == "R":
            return at >= 0
        if kind == "D":
            return at // 4 == tile
        if tile == 0:
            return (at == 0) if tree == 0 else (at < 3)
        return (at <= 4) if tree == 0 else (at < 7)

    def piece(kind, tile, tree, index, of=None):
        if kind == "R":
            rows = pl.ds(tree * 256 + index * DEEP, DEEP)
            return sides.at[:, tile, rows, :] if of is None else sides.at[of, tile, rows, :]
        if kind == "D":
            return inverses.at[y, tree * 64 : (tree + 1) * 64, :]
        if tile == 0:
            return slabs.at[0, y, 128:256, :] if tree == 0 else slabs.at[0, y, 256:512, :]
        return slabs.at[1, y, 0:256, :] if tree == 0 else slabs.at[1, y, 256:512, :]

    def slot_of(kind, index):
        return {"L": 0, "D": 1, "R": 2}[kind] + index

    first_of = (Z, X)
    second_of = (X, Z)

    def place_in(tile, tree):
        to_z = lax.rem(z - tile + RING, RING)
        return (to_z, x) if tree == 0 else (x, to_z)

    def roles(tile, tree):
        f, g = place_in(tile, tree)
        root = (f == 0) & (g == 0)
        late = (f == 0) & (g != 0)
        up_first = (g == 0) & (f <= 3)
        down_first = ((g == 0) & ((f == 0) | (f >= 6))) | ((f == 1) & (g != 0))
        up_second = (f != 0) & (g <= 3)
        down_second = (f != 0) & ((g == 0) | (g >= 6))
        return root, late, (up_first, down_first, up_second, down_second)

    def targets(tree):
        at = {X: x, Z: z}
        a, b = first_of[tree], second_of[tree]
        return [{a: around(at[a], 1)}, {a: around(at[a], -1)}, {b: around(at[b], 1)}, {b: around(at[b], -1)}]

    def plane_copy(kind, tile, tree, index, direction):
        ref = piece(kind, tile, tree, index)
        slot = slot_of(kind, index)
        return remote(
            ref, ref, plane_send.at[tile, tree, direction, slot], plane_recv.at[tile, tree, slot],
            targets(tree)[direction],
        )

    def hand_copy(kind, tile, tree, index):
        ref = piece(kind, tile, tree, index, of=RIDGE)
        slot = slot_of(kind, index)
        return remote(ref, ref, hand_send.at[tile, tree, slot], hand_recv.at[tile, tree, slot], mate)

    def hands(kind, root):
        return jnp.logical_not(root) if kind == "R" else (row >= 0)

    def relay(kind, index, late_turn):
        for tile in range(2):
            for tree in range(2):
                root, late, sends = roles(tile, tree)
                want = needed(kind, tile, tree, y)
                turn = late if late_turn else jnp.logical_not(late)

                @pl.when(want & turn)
                def _(tile=tile, tree=tree, root=root, sends=sends):
                    @pl.when(jnp.logical_not(root))
                    def _():
                        plane_copy(kind, tile, tree, index, 0).wait_recv()

                    if not late_turn:
                        for direction in range(4):

                            @pl.when(sends[direction])
                            def _(direction=direction):
                                plane_copy(kind, tile, tree, index, direction).start()

                    @pl.when(hands(kind, root))
                    def _():
                        hand_copy(kind, tile, tree, index).start()

    def drain(kind, index):
        for tile in range(2):
            for tree in range(2):
                root, late, sends = roles(tile, tree)
                want = needed(kind, tile, tree, y)
                for direction in range(4):

                    @pl.when(want & sends[direction])
                    def _(tile=tile, tree=tree, direction=direction):
                        plane_copy(kind, tile, tree, index, direction).wait_send()

                @pl.when(want & hands(kind, root))
                def _(tile=tile, tree=tree):
                    hand_copy(kind, tile, tree, index).wait_send()

    def p_ref(source, layer):
        return panel.at[source, layer * 512 : (layer + 1) * 512, :]

    def s_ref(unit, source):
        if unit == 0:
            return slabs.at[1, source, 0:256, :]
        if unit == 1:
            return slabs.at[1, source, 256:512, :]
        if unit == 2:
            return slabs.at[0, source, 256:512, :]
        if unit == 3:
            return slabs.at[0, source, 128:256, :]
        return inverses.at[source]

    UNIT = {0: ("L", 1, 0), 1: ("L", 1, 1), 2: ("L", 0, 1), 3: ("L", 0, 0)}

    def s_needed(unit, source):
        return needed(*UNIT[unit], source) if unit < 4 else (source >= 0)

    class Ring:
        def __init__(self, ref, wanted, send, recv, hand_s, hand_r):
            self.ref, self.wanted = ref, wanted
            self.send, self.recv, self.hand_s, self.hand_r = send, recv, hand_s, hand_r

        def hops(self, unit, way):
            return 4 if (unit % 2 == 0) == (way > 0) else 3

        def copy(self, unit, source, way, slot):
            ref = self.ref(unit, source)
            return remote(ref, ref, self.send.at[unit, slot], self.recv.at[unit, source], {Y: around(y, way)})

        def hand(self, unit, source):
            ref = self.ref(unit, source)
            return remote(ref, ref, self.hand_s.at[unit, source], self.hand_r.at[unit, source], mate)

        def open(self, unit):
            @pl.when(self.wanted(unit, y))
            def _():
                self.copy(unit, y, 1, y).start()
                self.copy(unit, y, -1, RING).start()

        def step(self, units, hop):
            for unit in units:
                for way in (1, -1):
                    if hop > self.hops(unit, way):
                        continue
                    source = around(y, -way * hop)

                    @pl.when(self.wanted(unit, source))
                    def _(unit=unit, way=way, source=source):
                        self.copy(unit, source, way, source).wait_recv()
                        if hop < self.hops(unit, way):
                            self.copy(unit, source, way, source).start()
                        self.hand(unit, source).start()

        def drain(self, units):
            for unit in units:

                @pl.when(self.wanted(unit, y))
                def _(unit=unit):
                    self.copy(unit, y, 1, y).wait_send()
                    self.copy(unit, y, -1, RING).wait_send()

                for way in (1, -1):
                    for hop in range(1, self.hops(unit, way) + 1):
                        source = around(y, -way * hop)

                        @pl.when(self.wanted(unit, source))
                        def _(unit=unit, way=way, hop=hop, source=source):
                            if hop < self.hops(unit, way):
                                self.copy(unit, source, way, source).wait_send()
                            self.hand(unit, source).wait_send()

        def collect(self, units):
            for unit in units:
                for by in range(1, RING):
                    source = around(y, by)

                    @pl.when(self.wanted(unit, source))
                    def _(unit=unit, source=source):
                        self.hand(unit, source).wait_recv()

    rows_ring = Ring(lambda unit, s: p_ref(s, unit), lambda unit, s: s >= 0, p_send, p_recv, p_hand_send, p_hand_recv)
    slab_ring = Ring(s_ref, s_needed, s_send, s_recv, s_hand_send, s_hand_recv)
    PU, SU = range(2), range(5)

    @pl.when(is_plane)
    def _():
        @pl.when(row < 2)
        def _():
            slabs[row, y] = panel[y, 0:512, :]
            sides[PLANE, row] = rhs[0]
            pair_side.wait_recv()

        pair_piv.wait_recv()

        order = [("L", 0), ("R", 0), ("D", 0)] + [("R", index) for index in range(1, ROUNDS)]
        for at in range(3):
            if order[at][0] == "D":

                @pl.when((row < 2) & (y // 4 == row))
                def _():
                    block = panel[y, pl.ds(pl.multiple_of((y % 4) * 128, 128), 128), :]
                    lane = iota((1, 64), 1)
                    both = [sibling_piv[0:1, :], piv[0:1, :]] if PLANE == 1 else [piv[0:1, :], sibling_piv[0:1, :]]
                    inverses[y] = invert_diagonal(block, jnp.concatenate(both, axis=1))

            relay(*order[at], False)

        def round_of(index, carry):
            relay("R", index, False)

            @pl.when(index == LAG)
            def _():
                relay("L", 0, True)
                relay("D", 0, True)

            @pl.when(index >= LAG)
            def _():
                relay("R", index - LAG, True)

            return carry

        lax.fori_loop(1, ROUNDS, round_of, 0)

        def late_round(index, carry):
            relay("R", index, True)
            return carry

        lax.fori_loop(ROUNDS - LAG, ROUNDS, late_round, 0)
        rows_ring.collect(PU)
        slab_ring.collect(SU)

    @pl.when(is_ridge)
    def _():
        pair_piv.wait_recv()

        @pl.when(row < 2)
        def _():
            sides[RIDGE, row] = rhs[0]

        for unit in PU:
            rows_ring.open(unit)
        for hop in range(1, 5):
            rows_ring.step(PU, hop)
        for unit in range(4):
            kind, tile, tree = UNIT[unit]

            @pl.when(needed(kind, tile, tree, y))
            def _(kind=kind, tile=tile, tree=tree):
                hand_copy(kind, tile, tree, 0).wait_recv()

            slab_ring.open(unit)
        for tile in range(2):

            @pl.when(needed("D", tile, 0, y))
            def _(tile=tile):
                hand_copy("D", tile, 0, 0).wait_recv()
                hand_copy("D", tile, 1, 0).wait_recv()

        slab_ring.open(4)
        for hop in range(1, 5):
            slab_ring.step(SU, hop)

        def take(index, carry):
            for tile in range(2):
                for tree in range(2):
                    root, _, _ = roles(tile, tree)

                    @pl.when(hands("R", root))
                    def _(tile=tile, tree=tree):
                        hand_copy("R", tile, tree, index).wait_recv()

            return carry

        lax.fori_loop(0, ROUNDS, take, 0)

    def lower(tile, top, bottom, left, right):
        return jnp.concatenate(
            [slabs[tile, tile * 4 + j, top * 128 : bottom * 128, :] for j in range(left, right)], axis=1
        )

    def stack(a, c, b):
        zero = jnp.zeros((a.shape[0], b.shape[1]), F32)
        return jnp.concatenate(
            [jnp.concatenate([a, zero], axis=1), jnp.concatenate([c, b], axis=1)], axis=0
        )

    def inverse_of(tile):
        d = [inverses[tile * 4 + j] for j in range(4)]
        c10 = -dot_both(d[1], dot_exact_left(lower(tile, 1, 2, 0, 1), d[0]))
        c32 = -dot_both(d[3], dot_exact_left(lower(tile, 3, 4, 2, 3), d[2]))
        a, b = stack(d[0], c10, d[1]), stack(d[2], c32, d[3])
        c = -dot_both(b, dot_exact_left(lower(tile, 2, 4, 0, 2), a))
        return a, b, c

    a0, b0, c0 = inverse_of(0)
    a1, b1, c1 = inverse_of(1)
    top = sides[core, 0, 0:256, :]
    bottom = sides[core, 0, 256:512, :]
    full[0:256, :] = dot_exact_right(a0, top)
    full[256:512, :] = dot_exact_right(c0, top) + dot_exact_right(b0, bottom)
    low[0:512, :] = full[0:512, :].astype(BF16)
    link = jnp.concatenate([slabs[1, j] for j in range(4)], axis=1)
    rest = sides[core, 1].astype(F32) - dot(link, low[0:512, :])
    full[512:768, :] = dot_both(a1, rest[0:256, :])
    full[768:1024, :] = dot_both(c1, rest[0:256, :]) + dot_both(b1, rest[256:512, :])
    low[512:1024, :] = full[512:1024, :].astype(BF16)

    def put(layer):
        return pltpu.make_async_copy(out.at[layer], out_hbm.at[layer], local_sem.at[3 + layer])

    for layer in range(2):
        for at in range(0, 512, 256):
            rows = slice(layer * 512 + at, layer * 512 + at + 256)
            left = jnp.concatenate([panel[j, rows, :] for j in range(RING)], axis=1)
            out[layer, at : at + 256, :] = rhs[layer, at : at + 256, :].astype(F32) - dot(left, low[...])
        if layer == 0:

            @pl.when(row == 0)
            def _():
                out[0] = full[0:512, :]

            @pl.when(row == 1)
            def _():
                out[0] = full[512:1024, :]

        put(layer).start()

    pair_panel.wait_send()
    pair_piv.wait_send()

    @pl.when((row < 2) & is_ridge)
    def _():
        pair_side.wait_send()

    @pl.when(is_plane)
    def _():
        drain("L", 0)
        drain("D", 0)

        def drain_round(index, carry):
            drain("R", index)
            return carry

        lax.fori_loop(0, ROUNDS, drain_round, 0)

    @pl.when(is_ridge)
    def _():
        rows_ring.drain(PU)
        slab_ring.drain(SU)

    put(0).wait()
    put(1).wait()


def on_device(rhs, panel, pivots):
    dma = pltpu.SemaphoreType.DMA
    slots = ROUNDS + 2
    anywhere = pl.BlockSpec(memory_space=pl.ANY)
    return pl.pallas_call(
        kernel,
        out_shape=jax.ShapeDtypeStruct(rhs.shape, F32),
        in_specs=[anywhere] * 3,
        out_specs=anywhere,
        scratch_shapes=[
            pltpu.VMEM((2, 512, 64), BF16),
            pltpu.VMEM((2, 512, 64), BF16),
            pltpu.VMEM((1, 64), F32),
            pltpu.VMEM((1, 64), F32),
            pltpu.VMEM((2, 512, 512), BF16),
            pltpu.VMEM((RING, 1024, 128), BF16),
            pltpu.VMEM((2, 2, 512, 512), BF16),
            pltpu.VMEM((2, RING, 512, 128), BF16),
            pltpu.VMEM((RING, 128, 128), F32),
            pltpu.VMEM((1024, 512), BF16),
            pltpu.VMEM((1024, 512), F32),
            pltpu.VMEM((2, 512, 512), F32),
            dma((5,)),
            dma((3,)),
            dma((3,)),
            dma((2, 2, 4, slots)),
            dma((2, 2, slots)),
            dma((2, 2, slots)),
            dma((2, 2, slots)),
            dma((2, RING + 1)),
            dma((2, RING)),
            dma((2, RING)),
            dma((2, RING)),
            dma((5, RING + 1)),
            dma((5, RING)),
            dma((5, RING)),
            dma((5, RING)),
        ],
        compiler_params=pltpu.CompilerParams(
            collective_id=0, has_side_effects=True, vmem_limit_bytes=40 * 1024 * 1024
        ),
    )(rhs, panel, pivots.reshape(1, 64))


def solution(mesh):
    torus = Mesh(mesh.devices.reshape(8, 8, 8, 2), (X, Z, Y, CORE))
    return jax.shard_map(
        on_device,
        mesh=torus,
        in_specs=(P(None, (X, Z), (Y, CORE)), P(None, (X, Z), (Y, CORE)), P((Y, CORE))),
        out_specs=P(None, (X, Z), (Y, CORE)),
        check_vma=False,
    )
```

time: 416 us -> 88.4 us (0.21)
  the two profiles are of different devices: /device:TPU:1 before, /device:TPU:8 now
where the time goes in v1:
time: 88.4 us; the launch traced here: 88.2 us
  Pallas kernels  83.9 us (95%)
  local copies, waits for them, and re-layouts  4.27 us (5%)
    pallas_call x1, Pallas kernels, on_device(): pl.pallas_call(kernel, out_shape=jax.ShapeDtypeStruct(rhs.shape, F32), in...  83.9 us
    unnamed x6, local copies, waits for them, and re-layouts  4.27 us

profile of v1, /device:TPU:8, one launch (start us, length us, event | category | flops | bytes accessed | tf_op | source)
XLA Modules:
  0.0 88.2 jit_solution(7049852035696546510)
XLA Ops:
  0.0 1.1 %copy.4.panel_hbm = bf16[2,512,64]{2,1,0:T(8,128)(2,1)S(1)} copy(bf16[2,512,64]{1,2,0:T(8,128)(2,1)} %param.4) | data formatting | bytes 262144 | tf_op args[1]
  1.1 0.0 copy-start
  1.1 1.2 %copy-done = bf16[2,512,512]{2,1,0:T(8,128)(2,1)S(1)} copy-done((bf16[2,512,512]{2,1,0:T(8,128)(2,1)S(1)}, bf16[2,512,512]{2,1,0:T(8,128)(2,1)}, u32[]{:S(2)}) %copy-start) | copy-done | bytes 1048600
  2.3 0.0 copy-start.1
  2.3 0.7 copy-done.1
  3.0 83.9 %shard_map.37 = f32[2,512,512]{2,1,0:T(8,128)S(1)} custom-call(bf16[2,512,512]{2,1,0:T(8,128)(2,1)S(1)} %copy-done, bf16[2,512,64]{2,1,0:T(8,128)(2,1)S(1)} %copy.4.panel_hbm, f32[1,64]{1,0:T(1,128)S(1)} %bitcast.1), custom_call_target="tpu_custom_call" | custom-call | tf_op jit(solution)/shard_map/pallas_call | solution.py:503
  86.8 1.3 %copy.6 = f32[2,512,512]{2,1,0:T(8,128)} copy(f32[2,512,512]{2,1,0:T(8,128)S(1)} %shard_map.37) | data formatting | bytes 4194304
Async XLA Ops:
  1.1 1.2 %copy-start = (bf16[2,512,512]{2,1,0:T(8,128)(2,1)S(1)}, bf16[2,512,512]{2,1,0:T(8,128)(2,1)}, u32[]{:S(2)}) copy-start(bf16[2,512,512]{2,1,0:T(8,128)(2,1)} %rhs_hbm.1) | copy-start | bytes 3145732
  2.3 0.7 copy-start.1

commit v2 on v1

v2 whole, which is shorter than its diff:
```python
import functools

import jax
import jax.numpy as jnp
from jax import lax
from jax.experimental import pallas as pl
from jax.experimental.pallas import tpu as pltpu
from jax.sharding import Mesh
from jax.sharding import PartitionSpec as P

MESH = pl.DeviceIdType.MESH
F32 = jnp.float32
BF16 = jnp.bfloat16
X, Z, Y, CORE = "row_0", "row_1", "col_0", "col_1"
RING = 8
PLANE, RIDGE = 1, 0
ROUNDS = 8
DEEP = 256 // ROUNDS
LAG = 2
ORDER = 3


def dot(a, b):
    return jnp.dot(a, b, preferred_element_type=F32)


def dot_turned(a, b):
    return lax.dot_general(a, b, (((0,), (0,)), ((), ())), preferred_element_type=F32)


def split(v):
    high = v.astype(BF16)
    return high, (v - high.astype(F32)).astype(BF16)


def dot_exact_left(a, b):
    high, low = split(b)
    return dot(a, high) + dot(a, low)


def dot_exact_right(a, b):
    high, low = split(a)
    return dot(high, b) + dot(low, b)


def dot_both(a, b):
    ah, al = split(a)
    bh, bl = split(b)
    return dot(ah, bh) + (dot(ah, bl) + dot(al, bh))


def iota(shape, dim):
    return lax.broadcasted_iota(jnp.int32, shape, dim)


def invert_diagonal(block, pivots):
    n, base = 128, 32
    rows, cols = iota((n, n), 0), iota((n, n), 1)
    raw = jnp.where(rows > cols, block.astype(F32), 0.0)
    inverse_row = 1.0 / pivots
    inverse_col = jnp.sum(jnp.where(rows == cols, inverse_row, 0.0), axis=1, keepdims=True)
    scaled = raw * inverse_col
    parts = []
    for at in range(0, n, base):
        lower = scaled[at : at + base, :]
        part = (iota((base, n), 0) + at == iota((base, n), 1)).astype(F32)
        for j in range(base - 1):
            part = part - lower[:, at + j : at + j + 1] * part[j : j + 1, :]
        parts.append(part)
    result = jnp.concatenate(parts, axis=0)
    inside = rows // base == cols // base
    result = jnp.where(inside, result, 0.0) * inverse_row
    size = base
    while size < n:
        below = (rows // size) % 2 == 1
        mask = below & (cols // size == rows // size - 1)
        link = jnp.where(mask, raw, 0.0).astype(BF16)
        result = result - dot_both(result, dot_exact_left(link, result))
        size *= 2
    return result


def kernel(
    rhs_hbm, panel_hbm, pivots_hbm, out,
    own, sibling_own, piv, sibling_piv, rhs, panel, sides, slabs, inverses, low, full,
    local_sem, pair_send, pair_recv,
    plane_send, plane_recv, hand_send, hand_recv,
    p_send, p_recv, p_hand_send, p_hand_recv,
    s_send, s_recv, s_hand_send, s_hand_recv,
):
    x, z, y, core = (lax.axis_index(name) for name in (X, Z, Y, CORE))
    row = x * RING + z
    is_plane = core == PLANE
    is_ridge = core == RIDGE

    def around(value, by):
        return lax.rem(value + by + RING, RING)

    def span(value):
        return jnp.minimum(value, RING - value)

    def remote(src, dst, send, recv, where):
        return pltpu.make_async_remote_copy(
            src_ref=src, dst_ref=dst, send_sem=send, recv_sem=recv, device_id=where, device_id_type=MESH
        )

    mate = {CORE: 1 - core}

    take_panel = pltpu.make_async_copy(panel_hbm, own, local_sem.at[0])
    take_piv = pltpu.make_async_copy(pivots_hbm, piv, local_sem.at[1])
    take_rhs = pltpu.make_async_copy(rhs_hbm, rhs, local_sem.at[2])
    take_panel.start()
    take_piv.start()
    take_rhs.start()
    barrier = pltpu.get_barrier_semaphore()
    pl.semaphore_signal(barrier, inc=1, device_id=mate, device_id_type=MESH)

    @pl.when(is_plane)
    def _():
        for by in (1, -1):
            pl.semaphore_signal(barrier, inc=1, device_id={X: around(x, by)}, device_id_type=MESH)
            pl.semaphore_signal(barrier, inc=1, device_id={Z: around(z, by)}, device_id_type=MESH)
        pl.semaphore_wait(barrier, 5)

    @pl.when(is_ridge)
    def _():
        for by in (1, -1):
            pl.semaphore_signal(barrier, inc=1, device_id={Y: around(y, by)}, device_id_type=MESH)
        pl.semaphore_wait(barrier, 3)

    take_panel.wait()
    pair_panel = remote(own, sibling_own, pair_send.at[0], pair_recv.at[0], mate)
    pair_panel.start()
    take_piv.wait()
    pair_piv = remote(piv, sibling_piv, pair_send.at[1], pair_recv.at[1], mate)
    pair_piv.start()
    take_rhs.wait()
    pair_side = remote(rhs.at[0], sides.at[RIDGE, row], pair_send.at[2], pair_recv.at[2], mate)
    pair_inverse = remote(inverses.at[y], inverses.at[y], pair_send.at[3], pair_recv.at[3], mate)

    @pl.when((row < 2) & is_ridge)
    def _():
        pair_side.start()

    pair_panel.wait_recv()
    lane, place = iota((64, 128), 1), iota((64, 128), 0)
    mine = (lane == place + core * 64).astype(BF16)
    theirs = (lane == place + (1 - core) * 64).astype(BF16)
    for layer in range(2):
        chip = (dot_turned(own[layer], mine) + dot_turned(sibling_own[layer], theirs)).astype(BF16)
        panel[y, layer * 512 : (layer + 1) * 512, :] = chip
    pair_piv.wait_recv()

    @pl.when(row < 2)
    def _():
        slabs[row, y] = panel[y, 0:512, :]
        sides[core, row] = rhs[0]

    def needed(kind, tile, tree, at):
        if kind == "R":
            return at >= 0
        if kind == "D":
            return at // 4 == tile
        if tile == 0:
            return (at == 0) if tree == 0 else (at < 3)
        return (at <= 4) if tree == 0 else (at < 7)

    def piece(kind, tile, tree, index, of=None):
        if kind == "R":
            rows = pl.ds(tree * 256 + index * DEEP, DEEP)
            return sides.at[:, tile, rows, :] if of is None else sides.at[of, tile, rows, :]
        if kind == "D":
            return inverses.at[y, tree * 64 : (tree + 1) * 64, :]
        if tile == 0:
            return slabs.at[0, y, 128:256, :] if tree == 0 else slabs.at[0, y, 256:512, :]
        return slabs.at[1, y, 0:256, :] if tree == 0 else slabs.at[1, y, 256:512, :]

    SLOT = {"L": 0, "D": 1, "R": 2}
    first_of = (Z, X)
    second_of = (X, Z)

    def roles(tile, tree):
        to_z = lax.rem(z - tile + RING, RING)
        f, g = (to_z, x) if tree == 0 else (x, to_z)
        root = (f == 0) & (g == 0)
        late = (f == 0) & (g != 0)
        up_first = (g == 0) & (f <= 3)
        down_first = ((g == 0) & ((f == 0) | (f >= 6))) | ((f == 1) & (g != 0))
        up_second = (f != 0) & (g <= 3)
        down_second = (f != 0) & ((g == 0) | (g >= 6))
        depth = span(f) + span(g) + jnp.where(late, 2, 0)
        return root, depth, (up_first, down_first, up_second, down_second)

    def targets(tree):
        at = {X: x, Z: z}
        a, b = first_of[tree], second_of[tree]
        return [{a: around(at[a], 1)}, {a: around(at[a], -1)}, {b: around(at[b], 1)}, {b: around(at[b], -1)}]

    def plane_copy(kind, tile, tree, index, direction):
        ref = piece(kind, tile, tree, index)
        slot = SLOT[kind] + index
        return remote(
            ref, ref, plane_send.at[tile, tree, direction, SLOT[kind]], plane_recv.at[tile, tree, slot],
            targets(tree)[direction],
        )

    def hand_copy(kind, tile, tree, index):
        ref = piece(kind, tile, tree, index, of=RIDGE)
        at = SLOT[kind]
        return remote(ref, ref, hand_send.at[tile, tree, at], hand_recv.at[tile, tree, at], mate)

    def all_rounds(tile, tree, way=None):
        rows = slice(tree * 256, (tree + 1) * 256)
        at = SLOT["R"]
        if way is None:
            ref = sides.at[RIDGE, tile, rows, :]
            return remote(ref, ref, hand_send.at[tile, tree, at], hand_recv.at[tile, tree, at], mate)
        ref = sides.at[:, tile, rows, :]
        return remote(ref, ref, plane_send.at[tile, tree, way, at], plane_recv.at[tile, tree, at], mate)

    def relay(kind, tile, tree, index, role):
        root, _, sends = role

        @pl.when(needed(kind, tile, tree, y))
        def _():
            @pl.when(jnp.logical_not(root))
            def _():
                plane_copy(kind, tile, tree, index, 0).wait_recv()

            for direction in range(4):

                @pl.when(sends[direction])
                def _(direction=direction):
                    plane_copy(kind, tile, tree, index, direction).start()

            @pl.when(jnp.logical_not(root))
            def _():
                hand_copy(kind, tile, tree, index).start()

    PU, SU, DU = 8, 7, 2

    def p_ref(unit, source):
        return panel.at[source, pl.ds(unit * 128, 128), :]

    def s_ref(unit, source):
        if unit < 4:
            return slabs.at[1, source, unit * 128 : (unit + 1) * 128, :]
        if unit < 7:
            return slabs.at[0, source, (unit - 3) * 128 : (unit - 2) * 128, :]
        return inverses.at[source, (unit - 7) * 64 : (unit - 6) * 64, :]

    def s_needed(unit, source):
        if unit < 4:
            return source < unit + 4 if unit else source < 4
        if unit < 7:
            return source < unit - 3
        return source >= 0

    def s_count(unit):
        return (unit + 4) if unit < 4 else (unit - 3) if unit < 7 else RING

    def beside(way):
        return {Y: around(y, way)}

    def p_copy(unit, source, way):
        ref = p_ref(unit, source)
        return remote(ref, ref, p_send, p_recv.at[unit, source], beside(way))

    def p_hand(unit, source):
        ref = p_ref(unit, source)
        return remote(ref, ref, p_hand_send, p_hand_recv, mate)

    def s_copy(unit, source, way, slot):
        ref = s_ref(unit, source)
        return remote(ref, ref, s_send.at[unit, slot], s_recv.at[unit, source], beside(way))

    def s_hand(unit, source):
        ref = s_ref(unit, source)
        return remote(ref, ref, s_hand_send.at[unit, source], s_hand_recv.at[unit], mate)

    def s_open(unit):
        @pl.when(s_needed(unit, y))
        def _():
            s_copy(unit, y, 1, y).start()
            s_copy(unit, y, -1, RING).start()

    def reach(unit, way):
        return 4 if (unit % 2 == 0) == (way > 0) else 3

    def s_step(units, hop):
        for unit in units:
            for way in (1, -1):
                if hop > reach(unit, way):
                    continue
                source = around(y, -way * hop)

                @pl.when(s_needed(unit, source))
                def _(unit=unit, way=way, source=source):
                    s_copy(unit, source, way, source).wait_recv()
                    if hop < reach(unit, way):
                        s_copy(unit, source, way, source).start()
                    s_hand(unit, source).start()

    def s_drain(units, hop):
        for unit in units:
            if hop == 0:

                @pl.when(s_needed(unit, y))
                def _(unit=unit):
                    s_copy(unit, y, 1, y).wait_send()
                    s_copy(unit, y, -1, RING).wait_send()

                continue
            for way in (1, -1):
                if hop > reach(unit, way):
                    continue
                source = around(y, -way * hop)

                @pl.when(s_needed(unit, source))
                def _(unit=unit, way=way, source=source):
                    if hop < reach(unit, way):
                        s_copy(unit, source, way, source).wait_send()
                    s_hand(unit, source).wait_send()

    def s_collect(unit):
        def wait(count):
            if unit < 7:
                ref = slabs.at[1, 0:count, 0:128, :]
            else:
                ref = inverses.at[0:count, 0:64, :]
            remote(ref, ref, s_hand_send.at[unit, 0], s_hand_recv.at[unit], mate).wait_recv()

        count, mine_too = s_count(unit), s_needed(unit, y)
        if count > 1:

            @pl.when(mine_too)
            def _():
                wait(count - 1)

        if count < RING:

            @pl.when(jnp.logical_not(mine_too))
            def _():
                wait(count)

    most = panel.at[0:7]

    @pl.when(is_plane)
    def _():
        @pl.when(row < 2)
        def _():
            pair_side.wait_recv()

        streams = [(tile, tree, roles(tile, tree)) for tile in range(2) for tree in range(2)]
        first = functools.reduce(jnp.minimum, [role[1] for _, _, role in streams])
        last = functools.reduce(jnp.maximum, [role[1] for _, _, role in streams])

        def turn(step, carry):
            for tile, tree, role in streams:
                at = step - LAG * role[1]

                @pl.when(at == 0)
                def _(tile=tile, tree=tree, role=role):
                    relay("L", tile, tree, 0, role)

                @pl.when(at == ORDER)
                def _(tile=tile, tree=tree, role=role):
                    if tree == 0:

                        @pl.when(role[0] & needed("D", tile, tree, y))
                        def _():
                            pair_inverse.wait_recv()

                    relay("D", tile, tree, 0, role)

                @pl.when((at > 0) & (at < ROUNDS + 2) & (at != ORDER))
                def _(tile=tile, tree=tree, role=role, at=at):
                    relay("R", tile, tree, at - jnp.where(at < ORDER, 1, 2), role)

            return carry

        lax.fori_loop(LAG * first, LAG * last + ROUNDS + 2, turn, 0)

        for tile, tree, (root, _, sends) in streams:
            for direction in range(4):

                @pl.when(sends[direction])
                def _(tile=tile, tree=tree, direction=direction):
                    for kind in "LD":

                        @pl.when(needed(kind, tile, tree, y))
                        def _(kind=kind):
                            plane_copy(kind, tile, tree, 0, direction).wait_send()

                    all_rounds(tile, tree, direction).wait_send()

            @pl.when(jnp.logical_not(root))
            def _(tile=tile, tree=tree):
                for kind in "LD":

                    @pl.when(needed(kind, tile, tree, y))
                    def _(kind=kind):
                        hand_copy(kind, tile, tree, 0).wait_send()

                all_rounds(tile, tree).wait_send()

        remote(most, most, p_hand_send, p_hand_recv, mate).wait_recv()
        for unit in range(SU + DU):
            s_collect(unit)

    @pl.when(is_ridge)
    def _():
        def p_open(unit, carry):
            p_copy(unit, y, 1).start()
            p_copy(unit, y, -1).start()
            return carry

        lax.fori_loop(0, PU, p_open, 0)

        @pl.when((row < 2) & (y // 4 == row))
        def _():
            block = panel[y, pl.ds(pl.multiple_of((y % 4) * 128, 128), 128), :]
            both = [sibling_piv[0:1, :], piv[0:1, :]] if PLANE == 0 else [piv[0:1, :], sibling_piv[0:1, :]]
            inverses[y] = invert_diagonal(block, jnp.concatenate(both, axis=1))
            pair_inverse.start()

        for hop in range(1, 5):

            def p_step(unit, carry, hop=hop):
                for way in (1, -1):
                    source = around(y, -way * hop)
                    far = (unit % 2 == 0) if way > 0 else (unit % 2 == 1)

                    def arrive(source=source):
                        p_copy(unit, source, way).wait_recv()
                        p_hand(unit, source).start()

                    if hop < 3:
                        p_copy(unit, source, way).wait_recv()
                        p_copy(unit, source, way).start()
                        p_hand(unit, source).start()
                    elif hop == 3:
                        p_copy(unit, source, way).wait_recv()

                        @pl.when(far)
                        def _(source=source, way=way):
                            p_copy(unit, source, way).start()

                        p_hand(unit, source).start()
                    else:

                        @pl.when(far)
                        def _(source=source, way=way):
                            p_copy(unit, source, way).wait_recv()
                            p_hand(unit, source).start()

                return carry

            lax.fori_loop(0, PU, p_step, 0)

        for tile, tree, units in ((1, 0, (0, 1)), (1, 1, (2, 3)), (0, 1, (5, 6)), (0, 0, (4,))):
            root = roles(tile, tree)[0]

            @pl.when(needed("L", tile, tree, y) & jnp.logical_not(root))
            def _(tile=tile, tree=tree):
                hand_copy("L", tile, tree, 0).wait_recv()

            for unit in units:
                s_open(unit)
        for hop in range(1, 6):
            if hop < 5:
                s_step(range(SU), hop)
            if hop == 1:
                for tree in range(2):
                    for tile in range(2):
                        root = roles(tile, tree)[0]

                        @pl.when(needed("D", tile, tree, y) & jnp.logical_not(root))
                        def _(tile=tile, tree=tree):
                            hand_copy("D", tile, tree, 0).wait_recv()

                    s_open(SU + tree)
            else:
                s_step(range(SU, SU + DU), hop - 1)
            if hop < 5:
                s_drain(range(SU), hop - 1)
            if 1 < hop:
                s_drain(range(SU, SU + DU), hop - 2)
        for tile in range(2):
            for tree in range(2):

                @pl.when(jnp.logical_not(roles(tile, tree)[0]))
                def _(tile=tile, tree=tree):
                    all_rounds(tile, tree).wait_recv()

    def lower(tile, top, bottom, left, right):
        return jnp.concatenate(
            [slabs[tile, tile * 4 + j, top * 128 : bottom * 128, :] for j in range(left, right)], axis=1
        )

    def stack(a, c, b):
        zero = jnp.zeros((a.shape[0], b.shape[1]), F32)
        return jnp.concatenate(
            [jnp.concatenate([a, zero], axis=1), jnp.concatenate([c, b], axis=1)], axis=0
        )

    def inverse_of(tile):
        d = [inverses[tile * 4 + j] for j in range(4)]
        c10 = -dot_both(d[1], dot_exact_left(lower(tile, 1, 2, 0, 1), d[0]))
        c32 = -dot_both(d[3], dot_exact_left(lower(tile, 3, 4, 2, 3), d[2]))
        a, b = stack(d[0], c10, d[1]), stack(d[2], c32, d[3])
        c = -dot_both(b, dot_exact_left(lower(tile, 2, 4, 0, 2), a))
        return a, b, c

    a0, b0, c0 = inverse_of(0)
    a1, b1, c1 = inverse_of(1)
    top = sides[core, 0, 0:256, :]
    bottom = sides[core, 0, 256:512, :]
    full[0:256, :] = dot_exact_right(a0, top)
    full[256:512, :] = dot_exact_right(c0, top) + dot_exact_right(b0, bottom)
    low[0:512, :] = full[0:512, :].astype(BF16)
    link = jnp.concatenate([slabs[1, j] for j in range(4)], axis=1)
    rest = sides[core, 1].astype(F32) - dot(link, low[0:512, :])
    full[512:768, :] = dot_both(a1, rest[0:256, :])
    full[768:1024, :] = dot_both(c1, rest[0:256, :]) + dot_both(b1, rest[256:512, :])
    low[512:1024, :] = full[512:1024, :].astype(BF16)

    for layer in range(2):
        for at in range(0, 512, 256):
            rows = slice(layer * 512 + at, layer * 512 + at + 256)
            left = jnp.concatenate([panel[j, rows, :] for j in range(RING)], axis=1)
            out[layer, at : at + 256, :] = rhs[layer, at : at + 256, :].astype(F32) - dot(left, low[...])

    @pl.when(row == 0)
    def _():
        out[0] = full[0:512, :]

    @pl.when(row == 1)
    def _():
        out[0] = full[512:1024, :]

    pair_panel.wait_send()
    pair_piv.wait_send()

    @pl.when(is_ridge)
    def _():
        @pl.when(row < 2)
        def _():
            pair_side.wait_send()

            @pl.when(y // 4 == row)
            def _():
                pair_inverse.wait_send()

        remote(most, most, p_send, p_hand_recv, mate).wait_send()
        remote(most, most, p_hand_send, p_hand_recv, mate).wait_send()
        s_drain(range(SU), 4)
        s_drain(range(SU, SU + DU), 4)


def on_device(rhs, panel, pivots):
    dma = pltpu.SemaphoreType.DMA
    slots = ROUNDS + 2
    far = pl.BlockSpec(memory_space=pltpu.HBM)
    return pl.pallas_call(
        kernel,
        out_shape=jax.ShapeDtypeStruct(rhs.shape, F32),
        in_specs=[far] * 3,
        out_specs=pl.BlockSpec(memory_space=pltpu.VMEM),
        scratch_shapes=[
            pltpu.VMEM((2, 64, 512), BF16),
            pltpu.VMEM((2, 64, 512), BF16),
            pltpu.VMEM((1, 64), F32),
            pltpu.VMEM((1, 64), F32),
            pltpu.VMEM((2, 512, 512), BF16),
            pltpu.VMEM((RING, 1024, 128), BF16),
            pltpu.VMEM((2, 2, 512, 512), BF16),
            pltpu.VMEM((2, RING, 512, 128), BF16),
            pltpu.VMEM((RING, 128, 128), F32),
            pltpu.VMEM((1024, 512), BF16),
            pltpu.VMEM((1024, 512), F32),
            dma((3,)),
            dma((4,)),
            dma((4,)),
            dma((2, 2, 4, 3)),
            dma((2, 2, slots)),
            dma((2, 2, 3)),
            dma((2, 2, 3)),
            dma,
            dma((8, RING)),
            dma,
            dma,
            dma((9, RING + 1)),
            dma((9, RING)),
            dma((9, RING)),
            dma((9,)),
        ],
        compiler_params=pltpu.CompilerParams(
            collective_id=0, has_side_effects=True, vmem_limit_bytes=40 * 1024 * 1024
        ),
    )(*(pltpu.with_memory_space_constraint(a, pltpu.HBM) for a in (rhs, jnp.swapaxes(panel, 1, 2), pivots.reshape(1, 64))))


def solution(mesh):
    torus = Mesh(mesh.devices.reshape(8, 8, 8, 2), (X, Z, Y, CORE))
    return jax.shard_map(
        on_device,
        mesh=torus,
        in_specs=(P(None, (X, Z), (Y, CORE)), P(None, (X, Z), (Y, CORE)), P((Y, CORE))),
        out_specs=P(None, (X, Z), (Y, CORE)),
        check_vma=False,
    )
```

time: 88.4 us -> 65.8 us (0.74)
  the two profiles are of different devices: /device:TPU:8 before, /device:TPU:1 now
where the time goes in v2:
time: 65.8 us; the launch traced here: 65.6 us
  Pallas kernels  64.3 us (98%)
  local copies, waits for them, and re-layouts  1.32 us (2%)
    pallas_call x1, Pallas kernels, on_device(): pl.pallas_call(kernel, out_shape=jax.ShapeDtypeStruct(rhs.shape, F32), in...  64.3 us
    unnamed x1, local copies, waits for them, and re-layouts  1.32 us

profile of v2, /device:TPU:1, one launch (start us, length us, event | category | flops | bytes accessed | tf_op | source)
XLA Modules:
  0.0 65.6 jit_solution(7908971240273835713)
XLA Ops:
  0.0 64.3 %shard_map.37 = f32[2,512,512]{2,1,0:T(8,128)S(1)} custom-call(bf16[2,512,512]{2,1,0:T(8,128)(2,1)} %rhs_hbm.1, bf16[2,64,512]{2,1,0:T(8,128)(2,1)} %bitcast.2, f32[1,64]{1,0:T(1,128)} %bitcast.3), custom_call_target="tpu_custom_call" | custom-call | tf_op jit(solution)/shard_map/pallas_call | solution.py:565
  64.3 1.3 %copy.5 = f32[2,512,512]{2,1,0:T(8,128)} copy(f32[2,512,512]{2,1,0:T(8,128)S(1)} %shard_map.37) | data formatting | bytes 4194304

commit v3 on v2

v3 whole, which is shorter than its diff:
```python
import functools

import jax
import jax.numpy as jnp
from jax import lax
from jax.experimental import pallas as pl
from jax.experimental.pallas import tpu as pltpu
from jax.sharding import Mesh
from jax.sharding import PartitionSpec as P

MESH = pl.DeviceIdType.MESH
F32 = jnp.float32
BF16 = jnp.bfloat16
X, Z, Y, CORE = "row_0", "row_1", "col_0", "col_1"
RING = 8
PLANE, RIDGE = 1, 0
ROUNDS = 8
DEEP = 256 // ROUNDS
LAG = 2


def dot(a, b):
    return jnp.dot(a, b, preferred_element_type=F32)


def dot_turned(a, b):
    return lax.dot_general(a, b, (((0,), (0,)), ((), ())), preferred_element_type=F32)


def split(v):
    high = v.astype(BF16)
    return high, (v - high.astype(F32)).astype(BF16)


def dot_exact_left(a, b):
    high, low = split(b)
    return dot(a, high) + dot(a, low)


def dot_exact_right(a, b):
    high, low = split(a)
    return dot(high, b) + dot(low, b)


def dot_both(a, b):
    ah, al = split(a)
    bh, bl = split(b)
    return dot(ah, bh) + (dot(ah, bl) + dot(al, bh))


def iota(shape, dim):
    return lax.broadcasted_iota(jnp.int32, shape, dim)


def invert_diagonal(block, pivots):
    n, base = 128, 32
    rows, cols = iota((n, n), 0), iota((n, n), 1)
    raw = jnp.where(rows > cols, block.astype(F32), 0.0)
    inverse_row = 1.0 / pivots
    inverse_col = jnp.sum(jnp.where(rows == cols, inverse_row, 0.0), axis=1, keepdims=True)
    scaled = raw * inverse_col
    parts = []
    for at in range(0, n, base):
        lower = scaled[at : at + base, :]
        part = (iota((base, n), 0) + at == iota((base, n), 1)).astype(F32)
        for j in range(base - 1):
            part = part - lower[:, at + j : at + j + 1] * part[j : j + 1, :]
        parts.append(part)
    result = jnp.concatenate(parts, axis=0)
    inside = rows // base == cols // base
    result = jnp.where(inside, result, 0.0) * inverse_row
    size = base
    while size < n:
        below = (rows // size) % 2 == 1
        mask = below & (cols // size == rows // size - 1)
        link = jnp.where(mask, raw, 0.0).astype(BF16)
        result = result - dot_both(result, dot_exact_left(link, result))
        size *= 2
    return result


def kernel(
    rhs_hbm, panel_hbm, pivots_hbm, out,
    own, sibling_own, piv, sibling_piv, rhs, panel, sides, slabs, inverses, low, full,
    ready, local_sem, pair_send, pair_recv,
    r_send, r_recv, r_hand_send, r_hand_recv,
    l_send, l_recv, l_hand_send, l_hand_recv,
    p_send, p_recv, p_hand_send, p_hand_recv,
    s_out, s_recv, s_hand_recv,
):
    x, z, y, core = (lax.axis_index(name) for name in (X, Z, Y, CORE))
    row = x * RING + z
    is_plane = core == PLANE
    is_ridge = core == RIDGE

    def around(value, by):
        return lax.rem(value + by + RING, RING)

    def span(value):
        return jnp.minimum(value, RING - value)

    def remote(src, dst, send, recv, where):
        return pltpu.make_async_remote_copy(
            src_ref=src, dst_ref=dst, send_sem=send, recv_sem=recv, device_id=where, device_id_type=MESH
        )

    mate = {CORE: 1 - core}

    take_panel = pltpu.make_async_copy(panel_hbm, own, local_sem.at[0])
    take_piv = pltpu.make_async_copy(pivots_hbm, piv, local_sem.at[1])
    take_rhs = pltpu.make_async_copy(rhs_hbm, rhs, local_sem.at[2])
    take_panel.start()
    take_piv.start()
    take_rhs.start()
    barrier = pltpu.get_barrier_semaphore()

    @pl.when(is_ridge)
    def _():
        for by in (1, -1):
            pl.semaphore_signal(barrier, inc=1, device_id={Y: around(y, by)}, device_id_type=MESH)
        pl.semaphore_wait(barrier, 3)
        pl.semaphore_signal(ready, inc=1, device_id=mate, device_id_type=MESH)

    @pl.when(is_plane)
    def _():
        pl.semaphore_signal(barrier, inc=1, device_id=mate, device_id_type=MESH)
        for by in (1, -1):
            pl.semaphore_signal(barrier, inc=1, device_id={X: around(x, by)}, device_id_type=MESH)
            pl.semaphore_signal(barrier, inc=1, device_id={Z: around(z, by)}, device_id_type=MESH)
        pl.semaphore_wait(ready, 1)

    take_panel.wait()
    pair_panel = remote(own, sibling_own, pair_send.at[0], pair_recv.at[0], mate)
    pair_panel.start()
    take_piv.wait()
    pair_piv = remote(piv, sibling_piv, pair_send.at[1], pair_recv.at[1], mate)
    pair_piv.start()
    take_rhs.wait()
    pair_side = remote(rhs.at[0], sides.at[RIDGE, row], pair_send.at[2], pair_recv.at[2], mate)

    @pl.when((row < 2) & is_ridge)
    def _():
        pair_side.start()

    pair_panel.wait_recv()
    lane, place = iota((64, 128), 1), iota((64, 128), 0)
    mine = (lane == place + core * 64).astype(BF16)
    theirs = (lane == place + (1 - core) * 64).astype(BF16)
    for layer in range(2):
        chip = (dot_turned(own[layer], mine) + dot_turned(sibling_own[layer], theirs)).astype(BF16)
        panel[y, layer * 512 : (layer + 1) * 512, :] = chip
    pair_piv.wait_recv()

    @pl.when(row < 2)
    def _():
        slabs[row, y] = panel[y, 0:512, :]
        sides[core, row] = rhs[0]

    BLOCKS = {(0, 0): (), (0, 1): (2, 3, 1, 0), (1, 0): (0, 1), (1, 1): (2, 3)}

    def l_needed(tile, block, at):
        return (at <= block) if tile == 0 else (at <= block + 4)

    first_of = (Z, X)
    second_of = (X, Z)

    def roles(tile, tree):
        to_z = lax.rem(z - tile + RING, RING)
        f, g = (to_z, x) if tree == 0 else (x, to_z)
        root = (f == 0) & (g == 0)
        late = (f == 0) & (g != 0)
        up_first = (g == 0) & (f <= 3)
        down_first = ((g == 0) & ((f == 0) | (f >= 6))) | ((f == 1) & (g != 0))
        up_second = (f != 0) & (g <= 3)
        down_second = (f != 0) & ((g == 0) | (g >= 6))
        depth = span(f) + span(g) + jnp.where(late, 2, 0)
        return root, depth, (up_first, down_first, up_second, down_second)

    def targets(tree):
        at = {X: x, Z: z}
        a, b = first_of[tree], second_of[tree]
        return [{a: around(at[a], 1)}, {a: around(at[a], -1)}, {b: around(at[b], 1)}, {b: around(at[b], -1)}]

    def r_ref(tile, tree, index, of):
        return sides.at[of, tile, pl.ds(tree * 256 + index * DEEP, DEEP), :]

    def r_copy(tile, tree, index, direction):
        ref = r_ref(tile, tree, index, slice(None))
        return remote(ref, ref, r_send.at[tile, tree], r_recv.at[tile, tree, index], targets(tree)[direction])

    def r_hand(tile, tree, index):
        ref = r_ref(tile, tree, index, RIDGE)
        return remote(ref, ref, r_hand_send.at[tile, tree], r_hand_recv.at[tile, tree], mate)

    def r_hand_all(tile, tree):
        ref = sides.at[RIDGE, tile, tree * 256 : (tree + 1) * 256, :]
        return remote(ref, ref, r_hand_send.at[tile, tree], r_hand_recv.at[tile, tree], mate)

    def l_ref(tile, block):
        return slabs.at[tile, y, block * 128 : (block + 1) * 128, :]

    def l_copy(tile, tree, block, direction):
        ref = l_ref(tile, block)
        return remote(ref, ref, l_send.at[tile, block], l_recv.at[tile, block], targets(tree)[direction])

    def l_hand(tile, block):
        ref = l_ref(tile, block)
        return remote(ref, ref, l_hand_send.at[tile, block], l_hand_recv.at[tile, block], mate)

    def relay(copy, hand, role):
        root, _, sends = role

        @pl.when(jnp.logical_not(root))
        def _():
            copy(0).wait_recv()

        for direction in range(4):

            @pl.when(sends[direction])
            def _(direction=direction):
                copy(direction).start()

        @pl.when(jnp.logical_not(root))
        def _():
            hand().start()

    PU, SU, DU = 4, 7, 2

    def p_ref(unit, source):
        return panel.at[source, pl.ds(unit * 256, 256), :]

    def s_ref(unit, source):
        if unit < 4:
            return slabs.at[1, source, unit * 128 : (unit + 1) * 128, :]
        if unit < 7:
            return slabs.at[0, source, (unit - 3) * 128 : (unit - 2) * 128, :]
        return inverses.at[source, (unit - 7) * 64 : (unit - 6) * 64, :]

    def s_needed(unit, source):
        if unit < 4:
            return source < unit + 4
        if unit < 7:
            return source < unit - 3
        return source >= 0

    def s_count(unit):
        return (unit + 4) if unit < 4 else (unit - 3) if unit < 7 else RING

    S_AT = [sum(s_count(before) for before in range(unit)) for unit in range(SU + DU)]

    def beside(way):
        return {Y: around(y, way)}

    def p_copy(unit, source, way):
        ref = p_ref(unit, source)
        return remote(ref, ref, p_send, p_recv.at[unit, source], beside(way))

    def p_hand(unit, source):
        ref = p_ref(unit, source)
        return remote(ref, ref, p_hand_send, p_hand_recv, mate)

    def turn_of(way):
        return 0 if way > 0 else 1

    def s_copy(unit, source, way, hop):
        ref = s_ref(unit, source)
        return remote(ref, ref, s_out.at[unit, turn_of(way), hop % 2], s_recv.at[S_AT[unit] + source], beside(way))

    def s_hand(unit, source, way, hop):
        ref = s_ref(unit, source)
        return remote(ref, ref, s_out.at[unit, turn_of(way), hop % 2], s_hand_recv.at[unit], mate)

    def s_sent(unit, way, hop, copies):
        ref = inverses.at[0, 0 : copies * 64, :] if unit >= SU else slabs.at[1, 0, 0 : copies * 128, :]
        remote(ref, ref, s_out.at[unit, turn_of(way), hop % 2], s_hand_recv.at[unit], mate).wait_send()

    def s_open(unit):
        @pl.when(s_needed(unit, y))
        def _():
            s_copy(unit, y, 1, 0).start()
            s_copy(unit, y, -1, 0).start()
            if unit >= SU:
                s_hand(unit, y, 1, 0).start()

    def reach(unit, way):
        return 4 if (unit % 2 == 0) == (way > 0) else 3

    def s_step(units, hop):
        arrivals = [
            (unit, way, around(y, -way * hop)) for unit in units for way in (1, -1) if hop <= reach(unit, way)
        ]
        for unit, way, source in arrivals:

            @pl.when(s_needed(unit, source))
            def _(unit=unit, way=way, source=source):
                s_copy(unit, source, way, hop).wait_recv()
                if hop < reach(unit, way):
                    s_copy(unit, source, way, hop).start()
                if hop == 4:
                    s_hand(unit, source, way, hop).start()

        if hop < 4:
            for unit, way, source in arrivals:

                @pl.when(s_needed(unit, source))
                def _(unit=unit, way=way, source=source):
                    s_hand(unit, source, way, hop).start()

    def s_drain(units, hop):
        for unit in units:
            for way in (1, -1):
                if hop > reach(unit, way):
                    continue
                source = around(y, -way * hop)

                @pl.when(s_needed(unit, source))
                def _(unit=unit, way=way):
                    if hop == 0:
                        s_sent(unit, way, hop, 2 if unit >= SU and way > 0 else 1)
                    else:
                        s_sent(unit, way, hop, 2 if hop < reach(unit, way) else 1)

    def s_collect(unit):
        def wait(count):
            if unit < 7:
                ref = slabs.at[1, 0:count, 0:128, :]
            else:
                ref = inverses.at[0:count, 0:64, :]
            remote(ref, ref, s_out.at[unit, 0, 0], s_hand_recv.at[unit], mate).wait_recv()

        if unit >= 7:
            wait(RING)
            return
        count, mine_too = s_count(unit), s_needed(unit, y)
        if count > 1:

            @pl.when(mine_too)
            def _():
                wait(count - 1)

        @pl.when(jnp.logical_not(mine_too))
        def _():
            wait(count)

    most = panel.at[0:7]

    @pl.when(is_plane)
    def _():
        pl.semaphore_wait(barrier, 4)

        @pl.when(row < 2)
        def _():
            pair_side.wait_recv()

        streams = [(tile, tree, roles(tile, tree)) for tile in range(2) for tree in range(2)]
        first = functools.reduce(jnp.minimum, [role[1] for _, _, role in streams])
        last = functools.reduce(jnp.maximum, [role[1] for _, _, role in streams])

        def turn(step, carry):
            for tile, tree, role in streams:
                at = step - LAG * role[1]

                @pl.when(at == 0)
                def _(tile=tile, tree=tree, role=role):
                    for block in BLOCKS[tile, tree]:

                        @pl.when(l_needed(tile, block, y))
                        def _(block=block):
                            relay(
                                lambda way: l_copy(tile, tree, block, way), lambda: l_hand(tile, block), role
                            )

                @pl.when((at > 0) & (at <= ROUNDS))
                def _(tile=tile, tree=tree, role=role, at=at):
                    relay(
                        lambda way: r_copy(tile, tree, at - 1, way), lambda: r_hand(tile, tree, at - 1), role
                    )

            return carry

        lax.fori_loop(LAG * first, LAG * last + ROUNDS + 1, turn, 0)

        for tile, tree, (root, _, sends) in streams:
            count = functools.reduce(jnp.add, [way.astype(jnp.int32) for way in sends])
            for copies in range(1, 5):

                @pl.when(count == copies)
                def _(tile=tile, tree=tree, copies=copies):
                    ref = panel.at[0 : 2 * copies]
                    remote(ref, ref, r_send.at[tile, tree], r_recv.at[tile, tree, 0], mate).wait_send()
                    for block in BLOCKS[tile, tree]:

                        @pl.when(l_needed(tile, block, y))
                        def _(block=block):
                            ref = panel.at[0, 0 : copies * 128, :]
                            remote(ref, ref, l_send.at[tile, block], l_recv.at[tile, block], mate).wait_send()

            @pl.when(jnp.logical_not(root))
            def _(tile=tile, tree=tree):
                r_hand_all(tile, tree).wait_send()
                for block in BLOCKS[tile, tree]:

                    @pl.when(l_needed(tile, block, y))
                    def _(block=block):
                        l_hand(tile, block).wait_send()

        remote(most, most, p_hand_send, p_hand_recv, mate).wait_recv()
        for unit in range(SU + DU):
            s_collect(unit)

    @pl.when(is_ridge)
    def _():
        def p_open(unit, carry):
            p_copy(unit, y, 1).start()
            p_copy(unit, y, -1).start()
            return carry

        lax.fori_loop(0, PU, p_open, 0)

        def p_step(hop):
            def step(unit, carry):
                for way in (1, -1):
                    source = around(y, -way * hop)
                    far = (unit % 2 == 0) if way > 0 else (unit % 2 == 1)

                    @pl.when(far | (hop < 4))
                    def _(source=source, way=way, far=far):
                        p_copy(unit, source, way).wait_recv()
                        if hop < 4:

                            @pl.when(far | (hop < 3))
                            def _():
                                p_copy(unit, source, way).start()

                        p_hand(unit, source).start()

                return carry

            lax.fori_loop(0, PU, step, 0)

        near = row == 0
        p_step(1)

        @pl.when(jnp.logical_not(near))
        def _():
            for hop in range(2, 5):
                p_step(hop)

        for tile, tree, opens in ((1, 0, {0: 0, 1: 1}), (1, 1, {2: 2, 3: 3}), (0, 1, {2: 5, 3: 6, 1: 4, 0: None})):
            root = roles(tile, tree)[0]
            for block in BLOCKS[tile, tree]:

                @pl.when(l_needed(tile, block, y) & jnp.logical_not(root))
                def _(tile=tile, block=block):
                    l_hand(tile, block).wait_recv()

                if opens[block] is not None:
                    s_open(opens[block])

        block = slabs[y // 4, y, pl.ds(pl.multiple_of((y % 4) * 128, 128), 128), :]
        both = [sibling_piv[0:1, :], piv[0:1, :]] if PLANE == 0 else [piv[0:1, :], sibling_piv[0:1, :]]
        inverses[y] = invert_diagonal(block, jnp.concatenate(both, axis=1))
        for unit in range(SU, SU + DU):
            s_open(unit)
        for hop in range(1, 5):
            s_step(range(SU), hop)
            s_step(range(SU, SU + DU), hop)
            s_drain(range(SU + DU), hop - 1)
            if hop < 4:

                @pl.when(near)
                def _(hop=hop):
                    p_step(hop + 1)

        for tile in range(2):
            for tree in range(2):

                @pl.when(jnp.logical_not(roles(tile, tree)[0]))
                def _(tile=tile, tree=tree):
                    r_hand_all(tile, tree).wait_recv()

    def lower(tile, top, bottom, left, right):
        return jnp.concatenate(
            [slabs[tile, tile * 4 + j, top * 128 : bottom * 128, :] for j in range(left, right)], axis=1
        )

    def stack(a, c, b):
        zero = jnp.zeros((a.shape[0], b.shape[1]), F32)
        return jnp.concatenate(
            [jnp.concatenate([a, zero], axis=1), jnp.concatenate([c, b], axis=1)], axis=0
        )

    def inverse_of(tile):
        d = [inverses[tile * 4 + j] for j in range(4)]
        c10 = -dot_both(d[1], dot_exact_left(lower(tile, 1, 2, 0, 1), d[0]))
        c32 = -dot_both(d[3], dot_exact_left(lower(tile, 3, 4, 2, 3), d[2]))
        a, b = stack(d[0], c10, d[1]), stack(d[2], c32, d[3])
        c = -dot_both(b, dot_exact_left(lower(tile, 2, 4, 0, 2), a))
        return a, b, c

    a0, b0, c0 = inverse_of(0)
    a1, b1, c1 = inverse_of(1)
    top = sides[core, 0, 0:256, :]
    bottom = sides[core, 0, 256:512, :]
    full[0:256, :] = dot_exact_right(a0, top)
    full[256:512, :] = dot_exact_right(c0, top) + dot_exact_right(b0, bottom)
    low[0:512, :] = full[0:512, :].astype(BF16)
    link = jnp.concatenate([slabs[1, j] for j in range(4)], axis=1)
    rest = sides[core, 1].astype(F32) - dot(link, low[0:512, :])
    full[512:768, :] = dot_both(a1, rest[0:256, :])
    full[768:1024, :] = dot_both(c1, rest[0:256, :]) + dot_both(b1, rest[256:512, :])
    low[512:1024, :] = full[512:1024, :].astype(BF16)

    for layer in range(2):
        for at in range(0, 512, 256):
            rows = slice(layer * 512 + at, layer * 512 + at + 256)
            left = jnp.concatenate([panel[j, rows, :] for j in range(RING)], axis=1)
            out[layer, at : at + 256, :] = rhs[layer, at : at + 256, :].astype(F32) - dot(left, low[...])

    @pl.when(row == 0)
    def _():
        out[0] = full[0:512, :]

    @pl.when(row == 1)
    def _():
        out[0] = full[512:1024, :]

    pair_panel.wait_send()
    pair_piv.wait_send()

    @pl.when(is_ridge)
    def _():
        @pl.when(row < 2)
        def _():
            pair_side.wait_send()

        remote(most, most, p_send, p_hand_recv, mate).wait_send()
        remote(most, most, p_hand_send, p_hand_recv, mate).wait_send()
        s_drain(range(SU + DU), 4)


def on_device(rhs, panel, pivots):
    dma = pltpu.SemaphoreType.DMA
    far = pl.BlockSpec(memory_space=pltpu.HBM)
    return pl.pallas_call(
        kernel,
        out_shape=jax.ShapeDtypeStruct(rhs.shape, F32),
        in_specs=[far] * 3,
        out_specs=pl.BlockSpec(memory_space=pltpu.VMEM),
        scratch_shapes=[
            pltpu.VMEM((2, 64, 512), BF16),
            pltpu.VMEM((2, 64, 512), BF16),
            pltpu.VMEM((1, 64), F32),
            pltpu.VMEM((1, 64), F32),
            pltpu.VMEM((2, 512, 512), BF16),
            pltpu.VMEM((RING, 1024, 128), BF16),
            pltpu.VMEM((2, 2, 512, 512), BF16),
            pltpu.VMEM((2, RING, 512, 128), BF16),
            pltpu.VMEM((RING, 128, 128), F32),
            pltpu.VMEM((1024, 512), BF16),
            pltpu.VMEM((1024, 512), F32),
            pltpu.SemaphoreType.REGULAR,
            dma((3,)),
            dma((3,)),
            dma((3,)),
            dma((2, 2)),
            dma((2, 2, ROUNDS)),
            dma((2, 2)),
            dma((2, 2)),
            dma((2, 4)),
            dma((2, 4)),
            dma((2, 4)),
            dma((2, 4)),
            dma,
            dma((4, RING)),
            dma,
            dma,
            dma((9, 2, 2)),
            dma((44,)),
            dma((9,)),
        ],
        compiler_params=pltpu.CompilerParams(
            collective_id=0, has_side_effects=True, vmem_limit_bytes=40 * 1024 * 1024
        ),
    )(*(pltpu.with_memory_space_constraint(a, pltpu.HBM) for a in (rhs, jnp.swapaxes(panel, 1, 2), pivots.reshape(1, 64))))


def solution(mesh):
    torus = Mesh(mesh.devices.reshape(8, 8, 8, 2), (X, Z, Y, CORE))
    return jax.shard_map(
        on_device,
        mesh=torus,
        in_specs=(P(None, (X, Z), (Y, CORE)), P(None, (X, Z), (Y, CORE)), P((Y, CORE))),
        out_specs=P(None, (X, Z), (Y, CORE)),
        check_vma=False,
    )
```

time: 65.8 us -> 53.7 us (0.82)
  the two profiles are of different devices: /device:TPU:1 before, /device:TPU:137 now
where the time goes in v3:
time: 53.7 us; the launch traced here: 53.5 us
  Pallas kernels  52.2 us (97%)
  local copies, waits for them, and re-layouts  1.32 us (2%)
    pallas_call x1, Pallas kernels, on_device(): pl.pallas_call(kernel, out_shape=jax.ShapeDtypeStruct(rhs.shape, F32), in...  52.2 us
    unnamed x1, local copies, waits for them, and re-layouts  1.32 us

profile of v3, /device:TPU:137, one launch (start us, length us, event | category | flops | bytes accessed | tf_op | source)
XLA Modules:
  0.0 53.5 jit_solution(9647829559282753526)
XLA Ops:
  0.0 52.2 %shard_map.37 = f32[2,512,512]{2,1,0:T(8,128)S(1)} custom-call(bf16[2,512,512]{2,1,0:T(8,128)(2,1)} %rhs_hbm.1, bf16[2,64,512]{2,1,0:T(8,128)(2,1)} %bitcast.2, f32[1,64]{1,0:T(1,128)} %bitcast.3), custom_call_target="tpu_custom_call" | custom-call | tf_op jit(solution)/shard_map/pallas_call | solution.py:545
  52.2 1.3 %copy.5 = f32[2,512,512]{2,1,0:T(8,128)} copy(f32[2,512,512]{2,1,0:T(8,128)S(1)} %shard_map.37) | data formatting | bytes 4194304

commit v4 on v3

--- a/solution.py
+++ b/solution.py
@@ -14,9 +14,9 @@
 X, Z, Y, CORE = "row_0", "row_1", "col_0", "col_1"
 RING = 8
 PLANE, RIDGE = 1, 0
-ROUNDS = 8
+ROUNDS = 16
 DEEP = 256 // ROUNDS
-LAG = 2
+NEAR, FAR = 3, 4
 
 
 def dot(a, b):
@@ -53,7 +53,7 @@
 
 
 def invert_diagonal(block, pivots):
-    n, base = 128, 32
+    n, base = 128, 16
     rows, cols = iota((n, n), 0), iota((n, n), 1)
     raw = jnp.where(rows > cols, block.astype(F32), 0.0)
     inverse_row = 1.0 / pivots
@@ -83,8 +83,8 @@
     rhs_hbm, panel_hbm, pivots_hbm, out,
     own, sibling_own, piv, sibling_piv, rhs, panel, sides, slabs, inverses, low, full,
     ready, local_sem, pair_send, pair_recv,
-    r_send, r_recv, r_hand_send, r_hand_recv,
-    l_send, l_recv, l_hand_send, l_hand_recv,
+    r_send, r_recv, r_hand_recv,
+    l_send, l_recv, l_hand_recv,
     p_send, p_recv, p_hand_send, p_hand_recv,
     s_out, s_recv, s_hand_recv,
 ):
@@ -135,12 +135,7 @@
     take_piv.wait()
     pair_piv = remote(piv, sibling_piv, pair_send.at[1], pair_recv.at[1], mate)
     pair_piv.start()
-    take_rhs.wait()
     pair_side = remote(rhs.at[0], sides.at[RIDGE, row], pair_send.at[2], pair_recv.at[2], mate)
-
-    @pl.when((row < 2) & is_ridge)
-    def _():
-        pair_side.start()
 
     pair_panel.wait_recv()
     lane, place = iota((64, 128), 1), iota((64, 128), 0)
@@ -149,14 +144,21 @@
     for layer in range(2):
         chip = (dot_turned(own[layer], mine) + dot_turned(sibling_own[layer], theirs)).astype(BF16)
         panel[y, layer * 512 : (layer + 1) * 512, :] = chip
-    pair_piv.wait_recv()
 
     @pl.when(row < 2)
     def _():
         slabs[row, y] = panel[y, 0:512, :]
-        sides[core, row] = rhs[0]
-
-    BLOCKS = {(0, 0): (), (0, 1): (2, 3, 1, 0), (1, 0): (0, 1), (1, 1): (2, 3)}
+
+    @pl.when(is_ridge)
+    def _():
+        take_rhs.wait()
+
+        @pl.when(row < 2)
+        def _():
+            pair_side.start()
+            sides[RIDGE, row] = rhs[0]
+
+    BLOCKS = {(0, 0): (), (0, 1): (0, 1, 2, 3), (1, 0): (0, 1), (1, 1): (2, 3)}
 
     def l_needed(tile, block, at):
         return (at <= block) if tile == 0 else (at <= block + 4)
@@ -190,11 +192,11 @@
 
     def r_hand(tile, tree, index):
         ref = r_ref(tile, tree, index, RIDGE)
-        return remote(ref, ref, r_hand_send.at[tile, tree], r_hand_recv.at[tile, tree], mate)
+        return remote(ref, ref, r_send.at[tile, tree], r_hand_recv.at[tile, tree], mate)
 
     def r_hand_all(tile, tree):
         ref = sides.at[RIDGE, tile, tree * 256 : (tree + 1) * 256, :]
-        return remote(ref, ref, r_hand_send.at[tile, tree], r_hand_recv.at[tile, tree], mate)
+        return remote(ref, ref, r_send.at[tile, tree], r_hand_recv.at[tile, tree], mate)
 
     def l_ref(tile, block):
         return slabs.at[tile, y, block * 128 : (block + 1) * 128, :]
@@ -205,7 +207,7 @@
 
     def l_hand(tile, block):
         ref = l_ref(tile, block)
-        return remote(ref, ref, l_hand_send.at[tile, block], l_hand_recv.at[tile, block], mate)
+        return remote(ref, ref, l_send.at[tile, block], l_hand_recv.at[tile, block], mate)
 
     def relay(copy, hand, role):
         root, _, sends = role
@@ -225,26 +227,22 @@
             hand().start()
 
     PU, SU, DU = 4, 7, 2
+    SLABS = ((1, 0, 4), (1, 1, 5), (1, 2, 6), (1, 3, 7), (0, 1, 1), (0, 2, 2), (0, 3, 3))
 
     def p_ref(unit, source):
         return panel.at[source, pl.ds(unit * 256, 256), :]
 
     def s_ref(unit, source):
-        if unit < 4:
-            return slabs.at[1, source, unit * 128 : (unit + 1) * 128, :]
-        if unit < 7:
-            return slabs.at[0, source, (unit - 3) * 128 : (unit - 2) * 128, :]
-        return inverses.at[source, (unit - 7) * 64 : (unit - 6) * 64, :]
+        if unit >= SU:
+            return inverses.at[source, (unit - SU) * 64 : (unit - SU + 1) * 64, :]
+        tile, block, _ = SLABS[unit]
+        return slabs.at[tile, source, block * 128 : (block + 1) * 128, :]
 
     def s_needed(unit, source):
-        if unit < 4:
-            return source < unit + 4
-        if unit < 7:
-            return source < unit - 3
-        return source >= 0
+        return source < s_count(unit)
 
     def s_count(unit):
-        return (unit + 4) if unit < 4 else (unit - 3) if unit < 7 else RING
+        return SLABS[unit][2] if unit < SU else RING
 
     S_AT = [sum(s_count(before) for before in range(unit)) for unit in range(SU + DU)]
 
@@ -271,7 +269,10 @@
         return remote(ref, ref, s_out.at[unit, turn_of(way), hop % 2], s_hand_recv.at[unit], mate)
 
     def s_sent(unit, way, hop, copies):
-        ref = inverses.at[0, 0 : copies * 64, :] if unit >= SU else slabs.at[1, 0, 0 : copies * 128, :]
+        if unit >= SU:
+            ref = inverses.at[0, 0 : copies * 64, :]
+        else:
+            ref = slabs.at[1, 0, 0 : copies * 128, :]
         remote(ref, ref, s_out.at[unit, turn_of(way), hop % 2], s_hand_recv.at[unit], mate).wait_send()
 
     def s_open(unit):
@@ -322,13 +323,13 @@
 
     def s_collect(unit):
         def wait(count):
-            if unit < 7:
+            if unit < SU:
                 ref = slabs.at[1, 0:count, 0:128, :]
             else:
                 ref = inverses.at[0:count, 0:64, :]
             remote(ref, ref, s_out.at[unit, 0, 0], s_hand_recv.at[unit], mate).wait_recv()
 
-        if unit >= 7:
+        if unit >= SU:
             wait(RING)
             return
         count, mine_too = s_count(unit), s_needed(unit, y)
@@ -347,18 +348,27 @@
     @pl.when(is_plane)
     def _():
         pl.semaphore_wait(barrier, 4)
-
-        @pl.when(row < 2)
-        def _():
-            pair_side.wait_recv()
+        pair_piv.wait_recv()
 
         streams = [(tile, tree, roles(tile, tree)) for tile in range(2) for tree in range(2)]
         first = functools.reduce(jnp.minimum, [role[1] for _, _, role in streams])
         last = functools.reduce(jnp.maximum, [role[1] for _, _, role in streams])
 
+        def by_count(count, root, sent):
+            @pl.when(root)
+            def _():
+                sent(2, 0)
+
+            for copies in range(4):
+
+                @pl.when((count == copies) & jnp.logical_not(root))
+                def _(copies=copies):
+                    sent(copies, 1)
+
         def turn(step, carry):
             for tile, tree, role in streams:
-                at = step - LAG * role[1]
+                at = step - NEAR * role[1]
+                index = step - FAR * role[1] - 1
 
                 @pl.when(at == 0)
                 def _(tile=tile, tree=tree, role=role):
@@ -370,39 +380,50 @@
                                 lambda way: l_copy(tile, tree, block, way), lambda: l_hand(tile, block), role
                             )
 
-                @pl.when((at > 0) & (at <= ROUNDS))
-                def _(tile=tile, tree=tree, role=role, at=at):
+                if BLOCKS[tile, tree]:
+
+                    @pl.when(index == ROUNDS // 2)
+                    def _(tile=tile, tree=tree, role=role):
+                        def sent(copies, hand):
+                            for block in BLOCKS[tile, tree]:
+
+                                @pl.when(l_needed(tile, block, y))
+                                def _(block=block):
+                                    ref = panel.at[0, 0 : (copies + hand) * 128, :]
+                                    remote(ref, ref, l_send.at[tile, block], l_recv.at[tile, block], mate).wait_send()
+
+                        by_count(functools.reduce(jnp.add, [way.astype(jnp.int32) for way in role[2]]), role[0], sent)
+
+                @pl.when((index >= 0) & (index < ROUNDS))
+                def _(tile=tile, tree=tree, role=role, index=index):
+                    if tree == 0:
+
+                        @pl.when(role[0] & (index == 0))
+                        def _():
+                            take_rhs.wait()
+                            sides[PLANE, row] = rhs[0]
+                            pair_side.wait_recv()
+
                     relay(
-                        lambda way: r_copy(tile, tree, at - 1, way), lambda: r_hand(tile, tree, at - 1), role
+                        lambda way: r_copy(tile, tree, index, way), lambda: r_hand(tile, tree, index), role
                     )
 
             return carry
 
-        lax.fori_loop(LAG * first, LAG * last + ROUNDS + 1, turn, 0)
+        lax.fori_loop(NEAR * first, FAR * last + ROUNDS + 1, turn, 0)
+
+        @pl.when(row >= 2)
+        def _():
+            take_rhs.wait()
 
         for tile, tree, (root, _, sends) in streams:
             count = functools.reduce(jnp.add, [way.astype(jnp.int32) for way in sends])
-            for copies in range(1, 5):
-
-                @pl.when(count == copies)
-                def _(tile=tile, tree=tree, copies=copies):
-                    ref = panel.at[0 : 2 * copies]
-                    remote(ref, ref, r_send.at[tile, tree], r_recv.at[tile, tree, 0], mate).wait_send()
-                    for block in BLOCKS[tile, tree]:
-
-                        @pl.when(l_needed(tile, block, y))
-                        def _(block=block):
-                            ref = panel.at[0, 0 : copies * 128, :]
-                            remote(ref, ref, l_send.at[tile, block], l_recv.at[tile, block], mate).wait_send()
-
-            @pl.when(jnp.logical_not(root))
-            def _(tile=tile, tree=tree):
-                r_hand_all(tile, tree).wait_send()
-                for block in BLOCKS[tile, tree]:
-
-                    @pl.when(l_needed(tile, block, y))
-                    def _(block=block):
-                        l_hand(tile, block).wait_send()
+
+            def sent(copies, hand, tile=tile, tree=tree):
+                ref = panel.at[0 : 2 * copies + hand]
+                remote(ref, ref, r_send.at[tile, tree], r_recv.at[tile, tree, 0], mate).wait_send()
+
+            by_count(count, root, sent)
 
         remote(most, most, p_hand_send, p_hand_recv, mate).wait_recv()
         for unit in range(SU + DU):
@@ -438,7 +459,28 @@
 
             lax.fori_loop(0, PU, step, 0)
 
+        tile, block = y // 4, y % 4
+
+        def invert_own():
+            @pl.when(row != tile)
+            def _():
+                ref = slabs.at[tile, y, pl.ds(block * 128, 128), :]
+                remote(ref, ref, l_send.at[tile, block], l_hand_recv.at[tile, block], mate).wait_recv()
+
+            diagonal = slabs[tile, y, pl.ds(pl.multiple_of(block * 128, 128), 128), :]
+            both = [sibling_piv[0:1, :], piv[0:1, :]] if PLANE == 0 else [piv[0:1, :], sibling_piv[0:1, :]]
+            inverses[y] = invert_diagonal(diagonal, jnp.concatenate(both, axis=1))
+            for unit in range(SU, SU + DU):
+                s_open(unit)
+
         near = row == 0
+        early = near & (tile == 0)
+        pair_piv.wait_recv()
+
+        @pl.when(early)
+        def _():
+            invert_own()
+
         p_step(1)
 
         @pl.when(jnp.logical_not(near))
@@ -446,31 +488,34 @@
             for hop in range(2, 5):
                 p_step(hop)
 
-        for tile, tree, opens in ((1, 0, {0: 0, 1: 1}), (1, 1, {2: 2, 3: 3}), (0, 1, {2: 5, 3: 6, 1: 4, 0: None})):
+        @pl.when(jnp.logical_not(early))
+        def _():
+            invert_own()
+
+        for tile, tree, opens in ((1, 0, {0: 0, 1: 1}), (1, 1, {2: 2, 3: 3}), (0, 1, {1: 4, 2: 5, 3: 6})):
             root = roles(tile, tree)[0]
             for block in BLOCKS[tile, tree]:
 
-                @pl.when(l_needed(tile, block, y) & jnp.logical_not(root))
+                @pl.when(l_needed(tile, block, y) & jnp.logical_not(root) & (y != tile * 4 + block))
                 def _(tile=tile, block=block):
                     l_hand(tile, block).wait_recv()
 
-                if opens[block] is not None:
+                if block in opens:
                     s_open(opens[block])
 
-        block = slabs[y // 4, y, pl.ds(pl.multiple_of((y % 4) * 128, 128), 128), :]
-        both = [sibling_piv[0:1, :], piv[0:1, :]] if PLANE == 0 else [piv[0:1, :], sibling_piv[0:1, :]]
-        inverses[y] = invert_diagonal(block, jnp.concatenate(both, axis=1))
-        for unit in range(SU, SU + DU):
-            s_open(unit)
+        @pl.when(near)
+        def _():
+            p_step(2)
+
         for hop in range(1, 5):
+            s_step(range(SU, SU + DU), hop)
             s_step(range(SU), hop)
-            s_step(range(SU, SU + DU), hop)
             s_drain(range(SU + DU), hop - 1)
-            if hop < 4:
+            if hop < 3:
 
                 @pl.when(near)
                 def _(hop=hop):
-                    p_step(hop + 1)
+                    p_step(hop + 2)
 
         for tile in range(2):
             for tree in range(2):
@@ -501,14 +546,13 @@
     a0, b0, c0 = inverse_of(0)
     a1, b1, c1 = inverse_of(1)
     top = sides[core, 0, 0:256, :]
-    bottom = sides[core, 0, 256:512, :]
     full[0:256, :] = dot_exact_right(a0, top)
-    full[256:512, :] = dot_exact_right(c0, top) + dot_exact_right(b0, bottom)
+    full[256:512, :] = dot_exact_right(jnp.concatenate([c0, b0], axis=1), sides[core, 0])
     low[0:512, :] = full[0:512, :].astype(BF16)
     link = jnp.concatenate([slabs[1, j] for j in range(4)], axis=1)
     rest = sides[core, 1].astype(F32) - dot(link, low[0:512, :])
     full[512:768, :] = dot_both(a1, rest[0:256, :])
-    full[768:1024, :] = dot_both(c1, rest[0:256, :]) + dot_both(b1, rest[256:512, :])
+    full[768:1024, :] = dot_both(jnp.concatenate([c1, b1], axis=1), rest)
     low[512:1024, :] = full[512:1024, :].astype(BF16)
 
     for layer in range(2):
@@ -566,8 +610,6 @@
             dma((2, 2)),
             dma((2, 2, ROUNDS)),
             dma((2, 2)),
-            dma((2, 2)),
-            dma((2, 4)),
             dma((2, 4)),
             dma((2, 4)),
             dma((2, 4)),

time: 53.7 us -> 52 us (0.968)
  the two profiles are of different devices: /device:TPU:137 before, /device:TPU:1 now
where the time goes in v4:
time: 52 us; the launch traced here: 51.7 us
  Pallas kernels  50.4 us (97%)
  local copies, waits for them, and re-layouts  1.32 us (3%)
    pallas_call x1, Pallas kernels, on_device(): pl.pallas_call(kernel, out_shape=jax.ShapeDtypeStruct(rhs.shape, F32), in...  50.4 us
    unnamed x1, local copies, waits for them, and re-layouts  1.32 us

profile of v4, /device:TPU:1, one launch (start us, length us, event | category | flops | bytes accessed | tf_op | source)
XLA Modules:
  0.0 51.7 jit_solution(8075771091799792969)
XLA Ops:
  0.0 50.4 %shard_map.37 = f32[2,512,512]{2,1,0:T(8,128)S(1)} custom-call(bf16[2,512,512]{2,1,0:T(8,128)(2,1)} %rhs_hbm.1, bf16[2,64,512]{2,1,0:T(8,128)(2,1)} %bitcast.2, f32[1,64]{1,0:T(1,128)} %bitcast.3), custom_call_target="tpu_custom_call" | custom-call | tf_op jit(solution)/shard_map/pallas_call | solution.py:589
  50.4 1.3 %copy.5 = f32[2,512,512]{2,1,0:T(8,128)} copy(f32[2,512,512]{2,1,0:T(8,128)S(1)} %shard_map.37) | data formatting | bytes 4194304

commit v5 on v4

--- a/solution.py
+++ b/solution.py
@@ -257,31 +257,21 @@
         ref = p_ref(unit, source)
         return remote(ref, ref, p_hand_send, p_hand_recv, mate)
 
-    def turn_of(way):
-        return 0 if way > 0 else 1
-
-    def s_copy(unit, source, way, hop):
+    def s_copy(unit, source, way):
         ref = s_ref(unit, source)
-        return remote(ref, ref, s_out.at[unit, turn_of(way), hop % 2], s_recv.at[S_AT[unit] + source], beside(way))
-
-    def s_hand(unit, source, way, hop):
+        return remote(ref, ref, s_out.at[2 if unit >= SU else 0], s_recv.at[S_AT[unit] + source], beside(way))
+
+    def s_hand(unit, source):
         ref = s_ref(unit, source)
-        return remote(ref, ref, s_out.at[unit, turn_of(way), hop % 2], s_hand_recv.at[unit], mate)
-
-    def s_sent(unit, way, hop, copies):
-        if unit >= SU:
-            ref = inverses.at[0, 0 : copies * 64, :]
-        else:
-            ref = slabs.at[1, 0, 0 : copies * 128, :]
-        remote(ref, ref, s_out.at[unit, turn_of(way), hop % 2], s_hand_recv.at[unit], mate).wait_send()
+        return remote(ref, ref, s_out.at[2 if unit >= SU else 1], s_hand_recv.at[unit], mate)
 
     def s_open(unit):
         @pl.when(s_needed(unit, y))
         def _():
-            s_copy(unit, y, 1, 0).start()
-            s_copy(unit, y, -1, 0).start()
+            s_copy(unit, y, 1).start()
+            s_copy(unit, y, -1).start()
             if unit >= SU:
-                s_hand(unit, y, 1, 0).start()
+                s_hand(unit, y).start()
 
     def reach(unit, way):
         return 4 if (unit % 2 == 0) == (way > 0) else 3
@@ -294,32 +284,41 @@
 
             @pl.when(s_needed(unit, source))
             def _(unit=unit, way=way, source=source):
-                s_copy(unit, source, way, hop).wait_recv()
+                s_copy(unit, source, way).wait_recv()
                 if hop < reach(unit, way):
-                    s_copy(unit, source, way, hop).start()
+                    s_copy(unit, source, way).start()
                 if hop == 4:
-                    s_hand(unit, source, way, hop).start()
+                    s_hand(unit, source).start()
 
         if hop < 4:
             for unit, way, source in arrivals:
 
                 @pl.when(s_needed(unit, source))
                 def _(unit=unit, way=way, source=source):
-                    s_hand(unit, source, way, hop).start()
-
-    def s_drain(units, hop):
-        for unit in units:
-            for way in (1, -1):
-                if hop > reach(unit, way):
-                    continue
-                source = around(y, -way * hop)
-
-                @pl.when(s_needed(unit, source))
-                def _(unit=unit, way=way):
-                    if hop == 0:
-                        s_sent(unit, way, hop, 2 if unit >= SU and way > 0 else 1)
-                    else:
-                        s_sent(unit, way, hop, 2 if hop < reach(unit, way) else 1)
+                    s_hand(unit, source).start()
+
+    def sent(count, slot):
+        ref = full.at[0 : count * 16, :]
+        remote(ref, ref, s_out.at[slot], s_hand_recv.at[0], mate).wait_send()
+
+    def s_drain():
+        sent(DU * (RING + RING - 1), 2)
+        for at in range(RING):
+            copies, hands = 0, 0
+            for unit in range(SU):
+                for source in range(s_count(unit)):
+                    if source == at:
+                        copies += 2
+                        continue
+                    up, down = (at - source) % RING, (source - at) % RING
+                    way, hop = (1, up) if up <= reach(unit, 1) else (-1, down)
+                    copies += hop < reach(unit, way)
+                    hands += 1
+
+            @pl.when(y == at)
+            def _(copies=copies, hands=hands):
+                sent(copies, 0)
+                sent(hands, 1)
 
     def s_collect(unit):
         def wait(count):
@@ -327,7 +326,7 @@
                 ref = slabs.at[1, 0:count, 0:128, :]
             else:
                 ref = inverses.at[0:count, 0:64, :]
-            remote(ref, ref, s_out.at[unit, 0, 0], s_hand_recv.at[unit], mate).wait_recv()
+            remote(ref, ref, s_out.at[0], s_hand_recv.at[unit], mate).wait_recv()
 
         if unit >= SU:
             wait(RING)
@@ -510,7 +509,6 @@
         for hop in range(1, 5):
             s_step(range(SU, SU + DU), hop)
             s_step(range(SU), hop)
-            s_drain(range(SU + DU), hop - 1)
             if hop < 3:
 
                 @pl.when(near)
@@ -580,7 +578,7 @@
 
         remote(most, most, p_send, p_hand_recv, mate).wait_send()
         remote(most, most, p_hand_send, p_hand_recv, mate).wait_send()
-        s_drain(range(SU + DU), 4)
+        s_drain()
 
 
 def on_device(rhs, panel, pivots):
@@ -617,7 +615,7 @@
             dma((4, RING)),
             dma,
             dma,
-            dma((9, 2, 2)),
+            dma((3,)),
             dma((44,)),
             dma((9,)),
         ],

time: 52 us -> 51.7 us (level)
  no operation moved by 1% of the time
where the time goes in v5:
time: 51.7 us; the launch traced here: 51.4 us
  Pallas kernels  50.1 us (97%)
  local copies, waits for them, and re-layouts  1.32 us (3%)
    pallas_call x1, Pallas kernels, on_device(): pl.pallas_call(kernel, out_shape=jax.ShapeDtypeStruct(rhs.shape, F32), in...  50.1 us
    unnamed x1, local copies, waits for them, and re-layouts  1.32 us

profile of v5, /device:TPU:1, one launch (start us, length us, event | category | flops | bytes accessed | tf_op | source)
XLA Modules:
  0.0 51.4 jit_solution(3041632314885340345)
XLA Ops:
  0.0 50.1 %shard_map.37 = f32[2,512,512]{2,1,0:T(8,128)S(1)} custom-call(bf16[2,512,512]{2,1,0:T(8,128)(2,1)} %rhs_hbm.1, bf16[2,64,512]{2,1,0:T(8,128)(2,1)} %bitcast.2, f32[1,64]{1,0:T(1,128)} %bitcast.3), custom_call_target="tpu_custom_call" | custom-call | tf_op jit(solution)/shard_map/pallas_call | solution.py:587
  50.1 1.3 %copy.5 = f32[2,512,512]{2,1,0:T(8,128)} copy(f32[2,512,512]{2,1,0:T(8,128)S(1)} %shard_map.37) | data formatting | bytes 4194304

commit v6 on v5

--- a/solution.py
+++ b/solution.py
@@ -118,7 +118,7 @@
     def _():
         for by in (1, -1):
             pl.semaphore_signal(barrier, inc=1, device_id={Y: around(y, by)}, device_id_type=MESH)
-        pl.semaphore_wait(barrier, 3)
+        pl.semaphore_wait(barrier, 5)
         pl.semaphore_signal(ready, inc=1, device_id=mate, device_id_type=MESH)
 
     @pl.when(is_plane)
@@ -127,6 +127,7 @@
         for by in (1, -1):
             pl.semaphore_signal(barrier, inc=1, device_id={X: around(x, by)}, device_id_type=MESH)
             pl.semaphore_signal(barrier, inc=1, device_id={Z: around(z, by)}, device_id_type=MESH)
+            pl.semaphore_signal(barrier, inc=1, device_id={Y: around(y, by), CORE: RIDGE}, device_id_type=MESH)
         pl.semaphore_wait(ready, 1)
 
     take_panel.wait()
@@ -265,6 +266,11 @@
         ref = s_ref(unit, source)
         return remote(ref, ref, s_out.at[2 if unit >= SU else 1], s_hand_recv.at[unit], mate)
 
+    def s_across(unit, source, way):
+        ref = s_ref(unit, source)
+        where = {Y: around(y, way), CORE: PLANE}
+        return remote(ref, ref, s_out.at[2 if unit >= SU else 0], s_hand_recv.at[unit], where)
+
     def s_open(unit):
         @pl.when(s_needed(unit, y))
         def _():
@@ -287,14 +293,14 @@
                 s_copy(unit, source, way).wait_recv()
                 if hop < reach(unit, way):
                     s_copy(unit, source, way).start()
-                if hop == 4:
-                    s_hand(unit, source).start()
-
-        if hop < 4:
-            for unit, way, source in arrivals:
+                    if hop + 1 == reach(unit, way):
+                        s_across(unit, source, way).start()
+
+        for unit, way, source in arrivals:
+            if hop < reach(unit, way):
 
                 @pl.when(s_needed(unit, source))
-                def _(unit=unit, way=way, source=source):
+                def _(unit=unit, source=source):
                     s_hand(unit, source).start()
 
     def sent(count, slot):
@@ -312,8 +318,8 @@
                         continue
                     up, down = (at - source) % RING, (source - at) % RING
                     way, hop = (1, up) if up <= reach(unit, 1) else (-1, down)
-                    copies += hop < reach(unit, way)
-                    hands += 1
+                    copies += (hop < reach(unit, way)) + (hop + 1 == reach(unit, way))
+                    hands += hop < reach(unit, way)
 
             @pl.when(y == at)
             def _(copies=copies, hands=hands):

time: 51.7 us -> 51.3 us (level)
  no operation moved by 1% of the time
where the time goes in v6:
time: 51.3 us; the launch traced here: 51.1 us
  Pallas kernels  49.7 us (97%)
  local copies, waits for them, and re-layouts  1.32 us (3%)
    pallas_call x1, Pallas kernels, on_device(): pl.pallas_call(kernel, out_shape=jax.ShapeDtypeStruct(rhs.shape, F32), in...  49.7 us
    unnamed x1, local copies, waits for them, and re-layouts  1.32 us

profile of v6, /device:TPU:1, one launch (start us, length us, event | category | flops | bytes accessed | tf_op | source)
XLA Modules:
  0.0 51.1 jit_solution(14183981849966949515)
XLA Ops:
  0.0 49.7 %shard_map.37 = f32[2,512,512]{2,1,0:T(8,128)S(1)} custom-call(bf16[2,512,512]{2,1,0:T(8,128)(2,1)} %rhs_hbm.1, bf16[2,64,512]{2,1,0:T(8,128)(2,1)} %bitcast.2, f32[1,64]{1,0:T(1,128)} %bitcast.3), custom_call_target="tpu_custom_call" | custom-call | tf_op jit(solution)/shard_map/pallas_call | solution.py:593
  49.7 1.3 %copy.5 = f32[2,512,512]{2,1,0:T(8,128)} copy(f32[2,512,512]{2,1,0:T(8,128)S(1)} %shard_map.37) | data formatting | bytes 4194304
